TPU v7x, 512 devices: a whole 4x8x8 slice. The times are simulated.
512 devices in a mesh: dp: 32 (over z, x), tensor: 16 (over y, core).
Axes of the slice: x: 4, y: 8, z: 8, core: 2. Of those that a mesh axis runs over, the one named last changes fastest.
Arguments:
- tokens: bfloat16 [4096, 4096], P('dp', 'tensor'), may hold values from -6 to 6
- out_grad: bfloat16 [4096, 4096], P('dp', 'tensor'), may hold values from -6 to 6
- up_weight: bfloat16 [4096, 14336], P('dp', 'tensor'), may hold values from -0.09375 to 0.09375
- down_weight: bfloat16 [14336, 4096], P('tensor', 'dp'), may hold values from -0.046875 to 0.046875
- up_accum: float32 [32, 256, 14336], P('dp', None, 'tensor'), may hold values from -6 to 6
- down_accum: float32 [32, 14336, 256], P('dp', 'tensor'), may hold values from -6 to 6
- up_q: float32 [14336, 32], P('tensor'), may hold values from -6 to 6
- down_q: float32 [256, 32], replicated, may hold values from -6 to 6
Outputs:
- input_grad: bfloat16 [4096, 4096], P('dp', 'tensor')
- up_error: float32 [32, 256, 14336], P('dp', None, 'tensor')
- up_left: float32 [256, 32], replicated
- up_right: float32 [14336, 32], P('tensor')
- down_error: float32 [32, 14336, 256], P('dp', 'tensor')
- down_left: float32 [14336, 32], P('tensor')
- down_right: float32 [256, 32], replicated
All inputs are finite; a program needn't handle non-finite values.
Results may differ from a plain program's by a relative error of at most 0.02.
Values may be sent and summed in bfloat16 or wider, within the bound.
A program may use at most 128 MiB of HBM per device.

v0:
```python
import math

import jax
import jax.numpy as jnp
from jax import lax
from jax.sharding import Mesh
from jax.sharding import PartitionSpec as P

DP = ("dp_0", "dp_1")


def side_by_side(arrays, axis, dim, along):
    both = jnp.concatenate(arrays, axis=along)
    filled, at, done = (lax.all_gather(both, axis, axis=dim, tiled=True), 0, [])
    for a in arrays:
        done.append(lax.slice_in_dim(filled, at, at + a.shape[along], axis=along))
        at += a.shape[along]
    return tuple(done)


def gather_axes(shard, axes, dim):
    filled = shard
    for number in range(len(axes) - 1, -1, -1):
        filled = lax.all_gather(filled, axes[number], axis=dim, tiled=True)
    return filled


def cut_along(shard, dim, count):
    before, after = (shard.shape[:dim], shard.shape[dim + 1 :])
    return jnp.moveaxis(shard.reshape(*before, count, -1, *after), dim, 0)


def summed_on_arrival(shard, axis, dim):
    pieces = cut_along(shard, dim, lax.axis_size(axis))
    arrived = lax.all_to_all(pieces, axis, split_axis=0, concat_axis=0, tiled=True)
    return arrived.astype(jnp.float32).sum(axis=0)


def over_pieces(shard, axis):
    return lax.all_gather(shard, axis).astype(jnp.float32).sum(0)


def filled_up(lines, count):
    spare = -lines.shape[0] % count
    if not spare:
        return lines
    return jnp.concatenate([lines, jnp.zeros((spare, *lines.shape[1:]), lines.dtype)])


def sent_to_all(shard, axis):
    count = lax.axis_size(axis)
    return lax.all_to_all(
        jnp.broadcast_to(shard[None], (count, *shard.shape)), axis, 0, 0, tiled=True
    )


def joined_along(pieces, dim):
    shape = list(pieces.shape[1:])
    shape[dim] *= pieces.shape[0]
    return jnp.moveaxis(pieces, 0, dim).reshape(shape)


def gather_directly(shard, axis, dim):
    pieces = sent_to_all(shard, axis)
    return joined_along(pieces, dim)


def total_of(shard, axes):
    lines = shard.reshape(-1, shard.shape[-1])
    padded = filled_up(lines, lax.axis_size(axes))
    whole = gather_directly(summed_on_arrival(padded, axes, 0).astype(jnp.bfloat16), axes, 0)
    return lax.slice_in_dim(whole, 0, len(lines)).reshape(shard.shape).astype(jnp.float32)


def over_copies(shard, axis):
    everything = sent_to_all(shard, axis)
    return jnp.sum(everything, axis=0)


def contract_first(left_arr, right_arr):
    return lax.dot_general(
        left_arr,
        right_arr,
        (((0,), (0,)), ((), ())),
        preferred_element_type=jnp.float32,
        precision=lax.Precision.HIGHEST,
    )


def contract_last(left_arr, right_arr):
    return lax.dot_general(
        left_arr, right_arr, (((1,), (1,)), ((), ())), preferred_element_type=jnp.float32
    )


def solve_rows(gram, left_rows):
    lower_factor = jnp.linalg.cholesky(gram)
    return lax.linalg.triangular_solve(
        lower_factor, left_rows, left_side=False, lower=True, transpose_a=True
    )


def shards(tokens, out_grad, up_weight, down_weight, up_accum, down_accum, up_q, down_q):
    highest = lax.Precision.HIGHEST
    full_tokens, full_grads = side_by_side((tokens, out_grad), "tensor", 1, 0)
    full_up = gather_axes(up_weight, DP, 0)
    preact = jnp.dot(full_tokens, full_up, preferred_element_type=jnp.float32)
    back_act = contract_last(full_grads, gather_axes(down_weight, DP, 1))
    squash = jax.nn.sigmoid(preact)
    act_out = (preact * squash).astype(jnp.bfloat16)
    hidden_grad = (back_act * squash * (1.0 + preact * (1.0 - squash))).astype(jnp.bfloat16)
    input_part = contract_last(hidden_grad, full_up)
    input_grad = summed_on_arrival(input_part.astype(jnp.bfloat16), "tensor", 1).astype(
        jnp.bfloat16
    )
    window = up_accum.shape[1]
    grad_scale = 1.0 / math.sqrt(tokens.shape[0])
    replicas = lax.axis_size(DP)
    up_matrix = up_accum[0] + contract_first(full_tokens[:, :window], hidden_grad) * grad_scale
    down_matrix = down_accum[0] + contract_first(act_out, full_grads[:, :window]) * grad_scale
    up_partial = jnp.dot(up_matrix, up_q, precision=highest)
    down_partial = jnp.dot(down_matrix, down_q, precision=highest)
    up_tensor = over_pieces(up_partial.astype(jnp.bfloat16), "tensor").astype(jnp.float32)
    up_sum, down_sum = (
        total_of(up_tensor.astype(jnp.bfloat16), DP),
        total_of(down_partial.astype(jnp.bfloat16), DP),
    )
    up_left = solve_rows(jnp.dot(up_sum.T, up_sum, precision=highest), up_sum)
    down_gram = over_copies(jnp.dot(down_sum.T, down_sum, precision=highest), "tensor")
    down_left = solve_rows(down_gram, down_sum)
    up_term = contract_first(up_matrix, up_left)
    down_term = contract_first(down_matrix, down_left)
    down_tensor = over_pieces(down_term.astype(jnp.bfloat16), "tensor").astype(jnp.float32)
    up_right, down_right = (
        total_of(up_term.astype(jnp.bfloat16), DP),
        total_of(down_tensor.astype(jnp.bfloat16), DP),
    )
    up_right = up_right / replicas
    down_right = down_right / replicas
    up_error = up_matrix - jnp.dot(up_left, up_right.T, precision=highest)
    down_error = down_matrix - jnp.dot(down_left, down_right.T, precision=highest)
    return (input_grad, up_error[None], up_left, up_right, down_error[None], down_left, down_right)


def solution(mesh):
    finer = Mesh(mesh.devices.reshape(8, 4, mesh.shape["tensor"]), ("dp_0", "dp_1", "tensor"))
    placed = (
        P(DP, "tensor"),
        P(DP, "tensor"),
        P(DP, "tensor"),
        P("tensor", DP),
        P(DP, None, "tensor"),
        P(DP, "tensor", None),
        P("tensor", None),
        P(),
    )
    return jax.shard_map(
        shards,
        mesh=finer,
        in_specs=placed,
        out_specs=(
            P(DP, "tensor"),
            P(DP, None, "tensor"),
            P(),
            P("tensor", None),
            P(DP, "tensor", None),
            P("tensor", None),
            P(),
        ),
        check_vma=False,
    )
```

profile of v0, /device:TPU:1, one launch (start us, length us, event | category | flops | bytes accessed | tf_op | source)
XLA Modules:
  0.0 462.0 jit_solution(8361467202445237362)
XLA Ops:
  8.8 14.3 %all_gather.30 = bf16[512,896]{1,0:T(8,128)(2,1)} all-gather(bf16[128,896]{1,0:T(8,128)(2,1)} %param.11), channel_id=1, replica_groups=mesh['dp_0'=8,'dp_1'=4,'tensor'=16] {'dp_1'}, dimensions={0}, use_global_device_ids=true | all-gather | bytes 1146880 | tf_op jit(solution)/shard_map/all_gather | solution.py:24
  23.3 14.1 %all_gather.28 = bf16[896,512]{1,0:T(8,128)(2,1)} all-gather(bf16[896,128]{1,0:T(8,128)(2,1)} %param.12), channel_id=1, replica_groups=mesh['dp_0'=8,'dp_1'=4,'tensor'=16] {'dp_1'}, dimensions={1}, use_global_device_ids=true | all-gather | bytes 1146880 | tf_op jit(solution)/shard_map/all_gather | solution.py:24
  37.4 22.3 %all-gather.6.cloned.1.call-done = bf16[256,4096]{1,0:T(8,128)(2,1)} async-done(((bf16[256,256]{1,0:T(8,128)(2,1)}), bf16[256,4096]{1,0:T(8,128)(2,1)}) %all-gather.6.cloned.1.call-update) | async-done | bytes 2097168 | tf_op jit(solution)/shard_map/all_gather | solution.py:14
  59.7 88.7 %all-gather.10.cloned.1.call-done = bf16[4096,896]{1,0:T(8,128)(2,1)} async-done(((bf16[512,896]{1,0:T(8,128)(2,1)}), bf16[4096,896]{1,0:T(8,128)(2,1)}) %all-gather.10.cloned.1.call-update) | async-done | bytes 7340048 | tf_op jit(solution)/shard_map/all_gather | solution.py:24
  148.4 4.7 %fusion.6 = f32[128,896]{1,0:T(8,128)S(1)} fusion(bf16[4096,896]{1,0:T(8,128)(2,1)} %all-gather.10.cloned.1.call-done, bf16[256,4096]{1,0:T(8,128)(2,1)} %all-gather.6.cloned.1.call-done), kind=kOutput, calls=%fused_computation.19 | convolution fusion | flops 939524096 | bytes 8847360 | tf_op jit(solution)/shard_map/dot_general | solution.py:107
  153.1 83.2 %all-gather.8.cloned.1.call-done = bf16[896,4096]{1,0:T(8,128)(2,1)} async-done(((bf16[896,512]{1,0:T(8,128)(2,1)}), bf16[896,4096]{1,0:T(8,128)(2,1)}) %all-gather.8.cloned.1.call-update) | async-done | bytes 7340048 | tf_op jit(solution)/shard_map/all_gather | solution.py:24
  236.3 5.9 %fusion.5 = bf16[128,896]{1,0:T(8,128)(2,1)S(1)} fusion(bf16[896,4096]{1,0:T(8,128)(2,1)} %all-gather.8.cloned.1.call-done, bf16[256,4096]{1,0:T(8,128)(2,1)} %all-gather.6.cloned.1.call-done, f32[128,896]{1,0:T(8,128)S(1)} %fusion.6), kind=kOutput, calls=%fused_computation.11 | convolution fusion | flops 940556288 | bytes 9076736 | tf_op jit(solution)/shard_map/dot_general | solution.py:91
  244.2 18.3 %all-gather = bf16[4096,32]{0,1:T(8,128)(2,1)S(1)} all-gather(bf16[256,32]{0,1:T(8,128)(2,1)S(1)} %convolution_convert_fusion.4), channel_id=2, replica_groups=mesh['dp_0'=8,'dp_1'=4,'tensor'=16] {'tensor'}, dimensions={0}, use_global_device_ids=true | all-gather | bytes 278528 | tf_op jit(solution)/shard_map/all_gather | solution.py:40
  263.6 6.7 %all-to-all-start.1 = ((bf16[32,2,128]{2,1,0:T(2,128)(2,1)}), bf16[32,2,128]{2,1,0:T(2,128)(2,1)S(1)}, u32[]{:S(2)}, u32[]{:S(2)}) async-start(bf16[32,2,128]{2,1,0:T(2,128)(2,1)} %reshape.71), calls=%async_computation.1 | async-start | bytes 32768 | tf_op jit(solution)/shard_map/all_to_all | solution.py:35
  271.8 7.0 %all-to-all-done.1 = bf16[32,2,128]{2,1,0:T(2,128)(2,1)S(1)} async-done(((bf16[32,2,128]{2,1,0:T(2,128)(2,1)}), bf16[32,2,128]{2,1,0:T(2,128)(2,1)S(1)}, u32[]{:S(2)}, u32[]{:S(2)}) %all-to-all-start.1) | async-done | bytes 16416 | tf_op jit(solution)/shard_map/all_to_all | solution.py:35
  286.1 5.9 %all-to-all-done.2 = bf16[32,2,128]{2,1,0:T(2,128)(2,1)S(1)} async-done(((bf16[32,2,128]{2,1,0:T(2,128)(2,1)}), bf16[32,2,128]{2,1,0:T(2,128)(2,1)S(1)}, u32[]{:S(2)}, u32[]{:S(2)}) %all-to-all-start.2) | async-done | bytes 16416 | tf_op jit(solution)/shard_map/all_to_all | solution.py:52
  292.1 3.9 all-to-all-start.5
  305.5 9.2 %all-to-all-start.3 = ((bf16[32,2,448]{2,1,0:T(2,128)(2,1)}), bf16[32,2,448]{2,1,0:T(2,128)(2,1)S(1)}, u32[]{:S(2)}, u32[]{:S(2)}) async-start(bf16[32,2,448]{2,1,0:T(2,128)(2,1)} %reshape.75), calls=%async_computation.3 | async-start | bytes 131072 | tf_op jit(solution)/shard_map/all_to_all | solution.py:35
  316.2 7.4 %all-to-all-done.3 = bf16[32,2,448]{2,1,0:T(2,128)(2,1)S(1)} async-done(((bf16[32,2,448]{2,1,0:T(2,128)(2,1)}), bf16[32,2,448]{2,1,0:T(2,128)(2,1)S(1)}, u32[]{:S(2)}, u32[]{:S(2)}) %all-to-all-start.3) | async-done | bytes 57376 | tf_op jit(solution)/shard_map/all_to_all | solution.py:35
  323.6 4.0 all-to-all-start.6
  328.0 8.5 %all-to-all-done.6 = bf16[32,2,448]{2,1,0:T(2,128)(2,1)S(1)} async-done(((bf16[32,2,448]{2,1,0:T(2,128)(2,1)}), bf16[32,2,448]{2,1,0:T(2,128)(2,1)S(1)}, u32[]{:S(2)}, u32[]{:S(2)}) %all-to-all-start.6) | async-done | bytes 57376 | tf_op jit(solution)/shard_map/all_to_all | solution.py:52
  337.7 10.1 %all-to-all-start.7 = ((f32[16,1,1024]{2,1,0:T(1,128)}), f32[16,1,1024]{2,1,0:T(1,128)S(1)}, u32[]{:S(2)}, u32[]{:S(2)}) async-start(f32[16,1,1024]{2,1,0:T(1,128)} %reshape.83), calls=%async_computation.7 | async-start | bytes 131072 | tf_op jit(solution)/shard_map/all_to_all | solution.py:52
  348.0 7.6 %all-to-all-done.7 = f32[16,1,1024]{2,1,0:T(1,128)S(1)} async-done(((f32[16,1,1024]{2,1,0:T(1,128)}), f32[16,1,1024]{2,1,0:T(1,128)S(1)}, u32[]{:S(2)}, u32[]{:S(2)}) %all-to-all-start.7) | async-done | bytes 65568 | tf_op jit(solution)/shard_map/all_to_all | solution.py:52
  364.9 15.4 %all-gather.1 = bf16[4096,32]{0,1:T(8,128)(2,1)S(1)} all-gather(bf16[256,32]{0,1:T(8,128)(2,1)S(1)} %convolution_convert_fusion.3), channel_id=3, replica_groups=mesh['dp_0'=8,'dp_1'=4,'tensor'=16] {'tensor'}, dimensions={0}, use_global_device_ids=true | all-gather | bytes 278528 | tf_op jit(solution)/shard_map/all_gather | solution.py:40
  386.2 7.6 %all-to-all-done.8 = bf16[32,2,128]{2,1,0:T(2,128)(2,1)S(1)} async-done(((bf16[32,2,128]{2,1,0:T(2,128)(2,1)}), bf16[32,2,128]{2,1,0:T(2,128)(2,1)S(1)}, u32[]{:S(2)}, u32[]{:S(2)}) %all-to-all-start.8) | async-done | bytes 16416 | tf_op jit(solution)/shard_map/all_to_all | solution.py:35
  398.5 8.0 %all-to-all-done.4 = bf16[32,2,448]{2,1,0:T(2,128)(2,1)S(1)} async-done(((bf16[32,2,448]{2,1,0:T(2,128)(2,1)}), bf16[32,2,448]{2,1,0:T(2,128)(2,1)S(1)}, u32[]{:S(2)}, u32[]{:S(2)}) %all-to-all-start.4) | async-done | bytes 57376 | tf_op jit(solution)/shard_map/all_to_all | solution.py:52
  410.3 5.5 %convolution_convert_fusion = bf16[128,4096]{1,0:T(8,128)(2,1)S(1)} fusion(bf16[128,896]{1,0:T(8,128)(2,1)S(1)} %fusion.5, bf16[4096,896]{1,0:T(8,128)(2,1)} %all-gather.10.cloned.1.call-done), kind=kOutput, calls=%fused_computation | convolution fusion | flops 940048384 | bytes 8617984 | tf_op jit(solution)/shard_map/dot_general | solution.py:91
  418.9 7.8 %all-to-all-start = ((bf16[16,128,256]{2,1,0:T(8,128)(2,1)}), bf16[16,128,256]{2,1,0:T(8,128)(2,1)S(1)}, u32[]{:S(2)}, u32[]{:S(2)}) async-start(bf16[16,128,256]{2,1,0:T(8,128)(2,1)} %bitcast.90), calls=%async_computation | async-start | bytes 2097152 | tf_op jit(solution)/shard_map/all_to_all | solution.py:35
  437.9 16.8 %all-to-all-done = bf16[16,128,256]{2,1,0:T(8,128)(2,1)S(1)} async-done(((bf16[16,128,256]{2,1,0:T(8,128)(2,1)}), bf16[16,128,256]{2,1,0:T(8,128)(2,1)S(1)}, u32[]{:S(2)}, u32[]{:S(2)}) %all-to-all-start) | async-done | bytes 1048608 | tf_op jit(solution)/shard_map/all_to_all | solution.py:35
  (101 shorter events, 64.9 us)
Async XLA Ops:
  7.2 236.2 %copy-start = (f32[896,32]{0,1:T(8,128)S(1)}, f32[896,32]{0,1:T(8,128)}, u32[]{:S(2)}) copy-start(f32[896,32]{0,1:T(8,128)} %param.15) | copy-start | bytes 344068
  7.2 52.5 %all-gather.6.cloned.1.call-start = ((), (), s32[]{:S(2)}) async-start(), calls=%async_computation.10 | async-start | bytes 2228224 | tf_op jit(solution)/shard_map/all_gather | solution.py:14
  8.8 139.6 %all-gather.10.cloned.1.call-start = ((), (), s32[]{:S(2)}) async-start(), calls=%async_computation.12 | async-start | bytes 8257536 | tf_op jit(solution)/shard_map/all_gather | solution.py:24
  23.2 213.1 %all-gather.8.cloned.1.call-start = ((), (), s32[]{:S(2)}) async-start(), calls=%async_computation.11 | async-start | bytes 8257536 | tf_op jit(solution)/shard_map/all_gather | solution.py:24
  153.1 89.1 %copy-start.2 = (f32[1,256,896]{2,1,0:T(8,128)S(1)}, f32[1,256,896]{2,1,0:T(8,128)}, u32[]{:S(2)}) copy-start(f32[1,256,896]{2,1,0:T(8,128)} %param.13) | copy-start | bytes 2752516
  153.1 130.4 %copy-start.5 = (f32[256,32]{0,1:T(8,128)S(1)}, f32[256,32]{0,1:T(8,128)}, u32[]{:S(2)}) copy-start(f32[256,32]{0,1:T(8,128)} %param.16) | copy-start | bytes 98308
  263.6 15.2 %all-to-all-start.1 = ((bf16[32,2,128]{2,1,0:T(2,128)(2,1)}), bf16[32,2,128]{2,1,0:T(2,128)(2,1)S(1)}, u32[]{:S(2)}, u32[]{:S(2)}) async-start(bf16[32,2,128]{2,1,0:T(2,128)(2,1)} %reshape.71), calls=%async_computation.1 | async-start | bytes 32768 | tf_op jit(solution)/shard_map/all_to_all | solution.py:35
  279.7 12.4 %all-to-all-start.2 = ((bf16[32,2,128]{2,1,0:T(2,128)(2,1)}), bf16[32,2,128]{2,1,0:T(2,128)(2,1)S(1)}, u32[]{:S(2)}, u32[]{:S(2)}) async-start(bf16[32,2,128]{2,1,0:T(2,128)(2,1)} %reshape.73), calls=%async_computation.2 | async-start | bytes 32768 | tf_op jit(solution)/shard_map/all_to_all | solution.py:52
  292.1 13.5 %all-to-all-start.5 = ((bf16[32,2,448]{2,1,0:T(2,128)(2,1)}), bf16[32,2,448]{2,1,0:T(2,128)(2,1)S(1)}, u32[]{:S(2)}, u32[]{:S(2)}) async-start(bf16[32,2,448]{2,1,0:T(2,128)(2,1)} %reshape.79), calls=%async_computation.5 | async-start | bytes 131072 | tf_op jit(solution)/shard_map/all_to_all | solution.py:35
  303.2 127.6 %copy-start.3 = (f32[256,32]{0,1:T(8,128)}, f32[256,32]{0,1:T(8,128)S(1)}, u32[]{:S(2)}) copy-start(f32[256,32]{0,1:T(8,128)S(1)} %fusion.12) | copy-start | bytes 98308
  305.5 18.0 %all-to-all-start.3 = ((bf16[32,2,448]{2,1,0:T(2,128)(2,1)}), bf16[32,2,448]{2,1,0:T(2,128)(2,1)S(1)}, u32[]{:S(2)}, u32[]{:S(2)}) async-start(bf16[32,2,448]{2,1,0:T(2,128)(2,1)} %reshape.75), calls=%async_computation.3 | async-start | bytes 131072 | tf_op jit(solution)/shard_map/all_to_all | solution.py:35
  323.6 12.9 %all-to-all-start.6 = ((bf16[32,2,448]{2,1,0:T(2,128)(2,1)}), bf16[32,2,448]{2,1,0:T(2,128)(2,1)S(1)}, u32[]{:S(2)}, u32[]{:S(2)}) async-start(bf16[32,2,448]{2,1,0:T(2,128)(2,1)} %reshape.81), calls=%async_computation.6 | async-start | bytes 131072 | tf_op jit(solution)/shard_map/all_to_all | solution.py:52
  337.7 17.9 %all-to-all-start.7 = ((f32[16,1,1024]{2,1,0:T(1,128)}), f32[16,1,1024]{2,1,0:T(1,128)S(1)}, u32[]{:S(2)}, u32[]{:S(2)}) async-start(f32[16,1,1024]{2,1,0:T(1,128)} %reshape.83), calls=%async_computation.7 | async-start | bytes 131072 | tf_op jit(solution)/shard_map/all_to_all | solution.py:52
  364.3 16.1 %copy-start.1 = (f32[896,32]{0,1:T(8,128)}, f32[896,32]{0,1:T(8,128)S(1)}, u32[]{:S(2)}) copy-start(f32[896,32]{0,1:T(8,128)S(1)} %fusion.17) | copy-start | bytes 344068
  381.4 12.4 %all-to-all-start.8 = ((bf16[32,2,128]{2,1,0:T(2,128)(2,1)}), bf16[32,2,128]{2,1,0:T(2,128)(2,1)S(1)}, u32[]{:S(2)}, u32[]{:S(2)}) async-start(bf16[32,2,128]{2,1,0:T(2,128)(2,1)} %reshape.85), calls=%async_computation.8 | async-start | bytes 32768 | tf_op jit(solution)/shard_map/all_to_all | solution.py:35
  393.7 12.7 %all-to-all-start.4 = ((bf16[32,2,448]{2,1,0:T(2,128)(2,1)}), bf16[32,2,448]{2,1,0:T(2,128)(2,1)S(1)}, u32[]{:S(2)}, u32[]{:S(2)}) async-start(bf16[32,2,448]{2,1,0:T(2,128)(2,1)} %reshape.77), calls=%async_computation.4 | async-start | bytes 131072 | tf_op jit(solution)/shard_map/all_to_all | solution.py:52
  406.5 12.4 %all-to-all-start.9 = ((bf16[32,2,128]{2,1,0:T(2,128)(2,1)}), bf16[32,2,128]{2,1,0:T(2,128)(2,1)S(1)}, u32[]{:S(2)}, u32[]{:S(2)}) async-start(bf16[32,2,128]{2,1,0:T(2,128)(2,1)} %reshape.87), calls=%async_computation.9 | async-start | bytes 32768 | tf_op jit(solution)/shard_map/all_to_all | solution.py:52
  418.9 8.2 %copy-start.4 = (bf16[32,2,128]{2,1,0:T(2,128)(2,1)}, bf16[32,2,128]{2,1,0:T(2,128)(2,1)S(1)}, u32[]{:S(2)}) copy-start(bf16[32,2,128]{2,1,0:T(2,128)(2,1)S(1)} %all-to-all-done.9) | copy-start | bytes 49156
  418.9 35.8 %all-to-all-start = ((bf16[16,128,256]{2,1,0:T(8,128)(2,1)}), bf16[16,128,256]{2,1,0:T(8,128)(2,1)S(1)}, u32[]{:S(2)}, u32[]{:S(2)}) async-start(bf16[16,128,256]{2,1,0:T(8,128)(2,1)} %bitcast.90), calls=%async_computation | async-start | bytes 2097152 | tf_op jit(solution)/shard_map/all_to_all | solution.py:35
Sparse Core Ops, SparseCore 0:
  10.6 49.0 all-gather.5
  61.8 86.5 all-gather.9
  150.5 85.7 all-gather.7
where the time goes:
time: 463 us; the launch traced here: 462 us
  waiting for transfers between devices  265 us (57%)
  blocking collectives  62.2 us (13%)
  starting transfers between devices  57.2 us (12%)
  matrix products  28.4 us (6%)
  other arithmetic  17.8 us (4%)
  local copies, waits for them, and re-layouts  17.4 us (4%)
  between operations  14.2 us (3%)
    all_gather x2, waiting for transfers between devices, gather_axes(): filled = lax.all_gather(filled, axes[number], axis=dim, tiled=True)  172 us
    all_to_all x5, waiting for transfers between devices, summed_on_arrival(): lax.all_to_all(pieces, axis, split_axis=0, concat_axis=0, tiled=True)  38.7 us
    all_gather x2, blocking collectives, over_pieces(): return lax.all_gather(shard, axis).astype(jnp.float32).sum(0)  33.8 us
    all_to_all x5, waiting for transfers between devices, sent_to_all(): lax.all_to_all(jnp.broadcast_to(shard[None], (count, *shard.shape)), axis...  32 us
    all_to_all x5, starting transfers between devices, summed_on_arrival(): lax.all_to_all(pieces, axis, split_axis=0, concat_axis=0, tiled=True)  31.4 us
    all_gather x2, blocking collectives, gather_axes(): filled = lax.all_gather(filled, axes[number], axis=dim, tiled=True)  28.4 us
    all_to_all x5, starting transfers between devices, sent_to_all(): lax.all_to_all(jnp.broadcast_to(shard[None], (count, *shard.shape)), axis...  25.7 us
    all_gather x1, waiting for transfers between devices, side_by_side(): filled, at, done = (lax.all_gather(both, axis, axis=dim, tiled=True), 0, [])  22.3 us
  transfers between devices with their start and end apart: 13, of which 12 were waited for; matrix products, arithmetic and copies ran while one was open for 9% of the time, Pallas kernels for 0%

commit v1 on v0

v1 whole, which is shorter than its diff:
```python
import functools
import math

import jax
import jax.numpy as jnp
from jax import lax
from jax.experimental import pallas as pl
from jax.experimental.pallas import tpu as pltpu
from jax.sharding import PartitionSpec as P

MESH = pl.DeviceIdType.MESH
HI = lax.Precision.HIGHEST
NZ, NX, NY = 8, 4, 8
NDP, NT = 32, 16
F32, BF16 = jnp.float32, jnp.bfloat16


def wrap(a, n):
    return lax.rem(a + 4 * n, n)


def dot_nt(a, b, precision=None):
    return lax.dot_general(
        a, b, (((1,), (1,)), ((), ())), preferred_element_type=F32, precision=precision
    )


def dot_nn(a, b, precision=None):
    return jnp.dot(a, b, preferred_element_type=F32, precision=precision)


def inverse_factor(gram):
    n = gram.shape[0]
    rows = lax.broadcasted_iota(jnp.int32, (n, 128), 0)
    lanes = lax.broadcasted_iota(jnp.int32, (n, 128), 1)
    unit = jnp.where(lanes == rows + n, 1.0, 0.0).astype(F32)
    work = jnp.concatenate([gram, jnp.zeros((n, 128 - n), F32)], axis=1) + unit
    for k in range(n):
        scale = lax.rsqrt(work[k : k + 1, k : k + 1])
        line = work[k : k + 1, :] * scale
        col = work[:, k : k + 1] * scale
        work = jnp.where(rows > k, work - col * line, jnp.where(rows == k, line, work))
    return work[:, n : 2 * n]


def kernel(
    tok, og, wu, wd, uq, dq, uacc, dacc,
    ig_out, ul_out, ur_out, dl_out, dr_out, uerr, derr,
    A, WU, WD, WIN, PF, SB, FB, RB, HG, IGP, IGX, PS, RY, FY, IGO, MU, MD,
    P28, R28, L28, P8, R8T, R8D, L8, GR,
    acc_sem, err_sem, ring_s, ring_r, xs, xr, ys, yr, ds, dr, ws, wr,
    rs_s, rs_r, hs, hr, ps_s, ps_r, ry_s, ry_r, fs, fr, cs, cr, gs, gr,
):
    dp, t = lax.axis_index("dp"), lax.axis_index("tensor")
    z, x = dp // NX, lax.rem(dp, NX)
    y, c = t // 2, lax.rem(t, 2)
    mine = x // 2 == c
    xl, xrr = wrap(x - 1, NX), wrap(x + 1, NX)
    sib = (dp, t + 1 - 2 * c)
    tokens = tok.shape[0]
    grad_scale = 1.0 / math.sqrt(tokens)

    def lanes_of(i):
        return pl.ds(pl.multiple_of(i * 128, 128), 128)

    def rcopy(src, dst, s, r, dev):
        return pltpu.make_async_remote_copy(
            src_ref=src, dst_ref=dst, send_sem=s, recv_sem=r, device_id=dev, device_id_type=MESH
        )

    def drain(ref, sem):
        pltpu.make_async_copy(ref, ref, sem).wait()

    def at_x(xi):
        return (z * NX + xi, t)

    load_u = pltpu.make_async_copy(uacc.at[0], MU, acc_sem.at[0])
    load_d = pltpu.make_async_copy(dacc.at[0], MD, acc_sem.at[1])
    load_u.start()
    load_d.start()

    WU[z] = wu[...]
    WD[:, lanes_of(z)] = wd[...]
    for h in range(2):

        @pl.when(jnp.logical_and(mine, lax.rem(x, 2) == h))
        def _():
            A[0, x, :, lanes_of(y)] = tok[:, h * 128 : (h + 1) * 128]
            A[1, x, :, lanes_of(y)] = og[:, h * 128 : (h + 1) * 128]

    @pl.when(t == 0)
    def _():
        WIN[0] = tok[...]
        WIN[1] = og[...]

    barrier = pltpu.get_barrier_semaphore()

    def greet_dp(j, carry):
        @pl.when(j != dp)
        def _():
            pl.semaphore_signal(barrier, inc=1, device_id=(j, t), device_id_type=MESH)

        return carry

    def greet_t(j, carry):
        @pl.when(j != t)
        def _():
            pl.semaphore_signal(barrier, inc=1, device_id=(dp, j), device_id_type=MESH)

        return carry

    lax.fori_loop(0, NDP, greet_dp, 0)
    lax.fori_loop(0, NT, greet_t, 0)

    @pl.when(jnp.logical_not(mine))
    def _():
        for h in range(2):
            pl.semaphore_signal(
                barrier,
                inc=1,
                device_id=(z * NX + 2 * c + h, 2 * y + x // 2),
                device_id_type=MESH,
            )

    pl.semaphore_wait(barrier, NDP + NT - 2 + 2 * jnp.where(mine, 0, 1).astype(jnp.int32))

    def slot(mat, zi, half):
        if mat == 0:
            return WU.at[zi, pl.ds(half * 64, 64)]
        return WD.at[pl.ds(half * 448, 448), lanes_of(zi)]

    def ring(mat, way, step, half):
        if way == 0:
            zi, to = wrap(z - step + 1, NZ), wrap(z + 1, NZ)
        else:
            zi, to = wrap(z + step - 1, NZ), wrap(z - 1, NZ)
        src = slot(mat, zi, half)
        if step == 1:
            src = wu.at[pl.ds(half * 64, 64)] if mat == 0 else wd.at[pl.ds(half * 448, 448)]
        i = (mat, way, half, step - 1)
        return rcopy(src, slot(mat, zi, half), ring_s.at[i], ring_r.at[i], (to * NX + x, t))

    def ring_arrived(mat, way, step, half):
        zi = wrap(z - step, NZ) if way == 0 else wrap(z + step, NZ)
        ref = slot(mat, zi, half)
        i = (mat, way, half, step - 1)
        rcopy(ref, ref, ring_s.at[i], ring_r.at[i], (dp, t)).wait_recv()

    def ring_parts(step):
        if step < 4:
            return [(way, half) for half in range(2) for way in range(2)]
        return [(0, 0), (1, 1)]

    def ring_send(mat, step, halves=(0, 1)):
        for way, half in ring_parts(step):
            if half in halves:
                ring(mat, way, step, half).start()

    def ring_pass(mat, step):
        nxt = ring_parts(step)
        for way, half in ring_parts(step - 1):
            ring_arrived(mat, way, step - 1, half)
            if (way, half) in nxt:
                ring(mat, way, step, half).start()

    def ring_end(mat):
        for way, half in ring_parts(4):
            ring_arrived(mat, way, 4, half)

    ring_send(0, 1)

    def piece(arr, h):
        xd = 2 * c + h
        src = (tok, og)[arr].at[:, pl.ds(h * 128, 128)]
        return rcopy(
            src,
            A.at[arr, x, :, lanes_of(y)],
            xs.at[arr, h],
            xr.at[arr, lax.rem(x, 2)],
            (z * NX + xd, 2 * y + x // 2),
        )

    def foreign(h):
        return jnp.logical_not(jnp.logical_and(mine, lax.rem(x, 2) == h))

    for arr in range(2):
        for h in range(2):

            @pl.when(foreign(h))
            def _():
                piece(arr, h).start()

    def pair(arr, yi):
        return A.at[arr, pl.ds(2 * c, 2), :, lanes_of(yi)]

    def spread(arr, off):
        yd = wrap(y + off, NY)
        return rcopy(pair(arr, y), pair(arr, y), ys.at[arr, off], yr.at[arr, off], (dp, 2 * yd + c))

    def to_sibling(arr, yi, off):
        return rcopy(pair(arr, yi), pair(arr, yi), ds.at[arr, off], dr.at[arr, off], sib)

    ring_send(1, 1, (0,))
    for arr in range(2):
        for h in range(2):

            @pl.when(foreign(h))
            def _():
                ref = A.at[arr, 2 * c + h, :, lanes_of(y)]
                rcopy(ref, ref, xs.at[arr, h], xr.at[arr, h], (dp, t)).wait_recv()

        for off in (4, 3, 5, 2, 6, 1, 7):
            spread(arr, off).start()
        to_sibling(arr, y, 0).start()

    @pl.when(t == 0)
    def _():
        def one(j, carry):
            rcopy(tok, WIN.at[0], ws.at[0], wr.at[0], (dp, j)).start()
            rcopy(og, WIN.at[1], ws.at[1], wr.at[1], (dp, j)).start()
            return carry

        lax.fori_loop(1, NT, one, 0)

    def y_arrivals(arr):
        for off in (1, 7, 2, 6, 3, 5, 4):
            yi = wrap(y - off, NY)
            ref = pair(arr, yi)
            rcopy(ref, ref, ys.at[arr, off], yr.at[arr, off], (dp, t)).wait_recv()
            to_sibling(arr, yi, off).start()

    def sibling_arrivals(arr):
        for off in range(NY):
            yi = wrap(y - off, NY)
            ref = A.at[arr, pl.ds(2 - 2 * c, 2), :, lanes_of(yi)]
            rcopy(ref, ref, ds.at[arr, off], dr.at[arr, off], (dp, t)).wait_recv()

    ring_pass(0, 2)
    ring_send(1, 1, (1,))
    ring_pass(0, 3)
    ring_pass(1, 2)
    ring_pass(0, 4)
    y_arrivals(0)
    ring_pass(1, 3)
    sibling_arrivals(0)
    ring_end(0)

    def products(mat):
        def one(d, carry):
            xi = wrap(x + d, NX)
            if mat == 0:
                PF[0, d] = dot_nn(A[0, xi], WU[...].reshape(NZ * 128, WU.shape[2]))
            else:
                PF[1, d] = dot_nt(A[1, xi], WD[...])
            return carry

        lax.fori_loop(0, NX, one, 0)

    half_rows = tokens // 2
    top, bot = pl.ds(0, half_rows), pl.ds(half_rows, half_rows)

    def rs_copy(mat, i):
        src = (SB.at[mat, 1, top], SB.at[mat, 1, bot], SB.at[mat, 0, bot],
               SB.at[mat, 2, top], SB.at[mat, 0, top], SB.at[mat, 2, bot])[i]
        dst = (FB.at[mat, 0], FB.at[mat, 1], RB.at[mat, 0, bot],
               RB.at[mat, 1, top], RB.at[mat, 0, top], RB.at[mat, 1, bot])[i]
        to = at_x(xrr if i % 2 == 0 else xl)
        return rcopy(src, dst, rs_s.at[mat, i], rs_r.at[mat, i], to)

    def rs_first(mat):
        SB[mat, 1] = PF[mat, 2].astype(BF16)
        rs_copy(mat, 0).start()
        rs_copy(mat, 1).start()
        SB[mat, 0, half_rows:] = PF[mat, 1, half_rows:].astype(BF16)
        rs_copy(mat, 2).start()
        SB[mat, 2, :half_rows] = PF[mat, 3, :half_rows].astype(BF16)
        rs_copy(mat, 3).start()

    def rs_second(mat):
        rs_copy(mat, 0).wait_recv()
        SB[mat, 0, :half_rows] = (PF[mat, 1, :half_rows] + FB[mat, 0].astype(F32)).astype(BF16)
        rs_copy(mat, 4).start()
        rs_copy(mat, 1).wait_recv()
        SB[mat, 2, half_rows:] = (PF[mat, 3, half_rows:] + FB[mat, 1].astype(F32)).astype(BF16)
        rs_copy(mat, 5).start()

    def rs_end(mat):
        for i in range(2, 6):
            rs_copy(mat, i).wait_recv()

    products(0)
    rs_first(0)
    y_arrivals(1)
    ring_pass(1, 4)
    rs_second(0)
    sibling_arrivals(1)
    ring_end(1)
    products(1)
    rs_first(1)
    rs_end(0)
    load_u.wait()
    load_d.wait()

    @pl.when(t != 0)
    def _():
        for arr in range(2):
            rcopy(WIN.at[arr], WIN.at[arr], ws.at[arr], wr.at[arr], (dp, t)).wait_recv()

    rs_second(1)
    rs_end(1)
    preact = PF[0, 0] + RB[0, 0].astype(F32) + RB[0, 1].astype(F32)
    back = PF[1, 0] + RB[1, 0].astype(F32) + RB[1, 1].astype(F32)
    squash = jax.nn.sigmoid(preact)
    act = (preact * squash).astype(BF16)
    hidden = (back * squash * (1.0 + preact * (1.0 - squash))).astype(BF16)
    HG[x] = hidden

    MU[...] += dot_nn(WIN[0].T, hidden) * grad_scale
    MD[...] += dot_nn(act.T, WIN[1]) * grad_scale

    def put28(k, arr):
        for g in range(4):
            for l in range(7):
                P28[k, g * 7 + l] = arr[8 * g : 8 * g + 8, 128 * l : 128 * l + 128]

    def put8(k, arr):
        for g in range(4):
            for l in range(2):
                P8[k, g * 2 + l] = arr[8 * g : 8 * g + 8, 128 * l : 128 * l + 128]

    def get(buf, k, n):
        return jnp.concatenate(
            [jnp.concatenate([buf[k, g * n + l] for l in range(n)], axis=1) for g in range(4)],
            axis=0,
        )

    def send28(k):
        def one(j, carry):
            @pl.when(j != dp)
            def _():
                rcopy(P28.at[k, j], R28.at[k, dp], cs.at[k, 0], cr.at[k, 0], (j, t)).start()

            return carry

        lax.fori_loop(0, 28, one, 0)

        @pl.when(dp < 28)
        def _():
            R28[k, dp] = P28[k, dp]

    def reduce28(k):
        @pl.when(dp < 28)
        def _():
            drain(R28.at[k, pl.ds(0, 31)], cr.at[k, 0])
            L28[k, dp] = jnp.sum(R28[k], axis=0)

            def one(j, carry):
                @pl.when(j != dp)
                def _():
                    rcopy(L28.at[k, dp], L28.at[k, dp], cs.at[k, 1], cr.at[k, 1], (j, t)).start()

                return carry

            lax.fori_loop(0, NDP, one, 0)

    def end28(k):
        @pl.when(dp < 28)
        def _():
            drain(L28.at[k, pl.ds(0, 27)], cr.at[k, 1])

        @pl.when(dp >= 28)
        def _():
            drain(L28.at[k, pl.ds(0, 28)], cr.at[k, 1])

    def send8(k):
        def one(j, carry):
            @pl.when(j != t)
            def _():
                rcopy(P8.at[k, j], R8T.at[k, t], cs.at[k, 2], cr.at[k, 2], (dp, j)).start()

            return carry

        lax.fori_loop(0, 8, one, 0)

        @pl.when(t < 8)
        def _():
            R8T[k, t] = P8[k, t]

    def middle8(k):
        @pl.when(t < 8)
        def _():
            drain(R8T.at[k, pl.ds(0, 15)], cr.at[k, 2])
            R8D[k, dp] = jnp.sum(R8T[k], axis=0)

            def one(j, carry):
                @pl.when(j != dp)
                def _():
                    rcopy(R8D.at[k, dp], R8D.at[k, dp], cs.at[k, 3], cr.at[k, 3], (j, t)).start()

                return carry

            lax.fori_loop(0, NDP, one, 0)

    def reduce8(k):
        @pl.when(t < 8)
        def _():
            drain(R8D.at[k, pl.ds(0, 31)], cr.at[k, 3])
            L8[k, t] = jnp.sum(R8D[k], axis=0)

            def one(j, carry):
                @pl.when(j != t)
                def _():
                    rcopy(L8.at[k, t], L8.at[k, t], cs.at[k, 4], cr.at[k, 4], (dp, j)).start()

                return carry

            lax.fori_loop(0, NT, one, 0)

    def end8(k):
        @pl.when(t < 8)
        def _():
            drain(L8.at[k, pl.ds(0, 7)], cr.at[k, 4])

        @pl.when(t >= 8)
        def _():
            drain(L8.at[k, pl.ds(0, 8)], cr.at[k, 4])

    put8(0, dot_nn(MU[...], uq[...], HI).T)
    send8(0)
    put28(0, dot_nn(MD[...], dq[...], HI).T)
    send28(0)

    def h_copy(i):
        own = HG.at[x]
        src = (own, own, HG.at[xl, top], HG.at[xrr, bot])[i]
        return rcopy(src, src, hs.at[i], hr.at[i], at_x(xrr if i % 2 == 0 else xl))

    def h_wait(i):
        x2 = wrap(x + 2, NX)
        ref = (HG.at[xl], HG.at[xrr], HG.at[x2, top], HG.at[x2, bot])[i]
        rcopy(ref, ref, hs.at[i], hr.at[i], (dp, t)).wait_recv()

    h_copy(0).start()
    h_copy(1).start()
    middle8(0)
    reduce28(0)
    h_wait(0)
    h_copy(2).start()
    h_wait(1)
    h_copy(3).start()
    reduce8(0)

    end28(0)
    down_sum = get(L28, 0, 7)
    put8(1, dot_nn(down_sum, MD[...], HI))
    send8(1)
    gram_part = dot_nt(down_sum, down_sum, HI)
    GR[t] = jnp.concatenate([gram_part[8 * g : 8 * g + 8] for g in range(4)], axis=1)

    def gram_send(j, carry):
        @pl.when(j != t)
        def _():
            rcopy(GR.at[t], GR.at[t], gs.at[0], gr.at[0], (dp, j)).start()

        return carry

    lax.fori_loop(0, NT, gram_send, 0)

    end8(0)
    up_sum = get(L8, 0, 2)
    put28(1, dot_nn(up_sum, MU[...], HI))
    send28(1)

    h_wait(2)
    h_wait(3)

    def ig_one(i, carry):
        IGP[i] = dot_nt(HG[i], WU[...].reshape(NZ * 128, WU.shape[2])).astype(BF16)
        return carry

    lax.fori_loop(0, NX, ig_one, 0)
    other = IGP.at[pl.ds(2 - 2 * c, 2)]
    pair_copy = rcopy(other, IGX, ps_s.at[0], ps_r.at[0], sib)
    pair_copy.start()

    middle8(1)
    up_inv = inverse_factor(dot_nt(up_sum, up_sum, HI))
    up_left_t = dot_nn(up_inv, up_sum, HI)
    up_left = up_left_t.T
    ul_out[...] = up_left
    reduce28(1)

    pair_copy.wait_recv()
    for i in range(2):
        both = (IGP[2 * c + i].astype(F32) + IGX[i].astype(F32)).astype(BF16)
        for k in range(NY):
            PS[k, i] = both[:, k * 128 : (k + 1) * 128]
    RY[y] = PS[y]

    def ry_send(j, carry):
        @pl.when(j != y)
        def _():
            rcopy(PS.at[j], RY.at[y], ry_s.at[0], ry_r.at[0], (dp, 2 * j + c)).start()

        return carry

    lax.fori_loop(0, NY, ry_send, 0)

    reduce8(1)
    drain(GR.at[pl.ds(0, NT - 1)], gr.at[0])
    packed = jnp.sum(GR[...], axis=0)
    gram = jnp.concatenate([packed[:, 32 * g : 32 * g + 32] for g in range(4)], axis=0)
    down_inv = inverse_factor(gram)
    down_left = dot_nn(down_inv, down_sum, HI).T
    dl_out[...] = down_left

    end28(1)
    up_right_t = dot_nn(up_inv, get(L28, 1, 7), HI) * (1.0 / NDP)
    ur_out[...] = up_right_t.T
    MU[...] -= dot_nn(up_left, up_right_t, HI)
    store_u = pltpu.make_async_copy(MU, uerr.at[0], err_sem.at[0])
    store_u.start()

    end8(1)
    down_right_t = dot_nn(down_inv, get(L8, 1, 2), HI) * (1.0 / NDP)
    dr_out[...] = down_right_t.T
    MD[...] -= dot_nn(down_left, down_right_t, HI)
    store_d = pltpu.make_async_copy(MD, derr.at[0], err_sem.at[1])
    store_d.start()

    drain(RY.at[pl.ds(0, NY - 1)], ry_r.at[0])
    for i in range(2):
        FY[i] = jnp.sum(RY[:, i].astype(F32), axis=0).astype(BF16)

    def last(i, h):
        return rcopy(
            FY.at[i],
            IGO.at[h],
            fs.at[i],
            fr.at[h],
            (z * NX + 2 * c + i, 2 * y + x // 2),
        )

    for h in range(2):
        for i in range(2):

            @pl.when(jnp.logical_and(lax.rem(x, 2) == h, foreign(i)))
            def _():
                last(i, h).start()

        @pl.when(jnp.logical_and(mine, lax.rem(x, 2) == h))
        def _():
            IGO[h] = FY[h]

    for h in range(2):

        @pl.when(foreign(h))
        def _():
            rcopy(IGO.at[h], IGO.at[h], fs.at[h], fr.at[h], (dp, t)).wait_recv()

        ig_out[:, h * 128 : (h + 1) * 128] = IGO[h]

    for mat in range(2):
        for step in range(1, 5):
            for way, half in ring_parts(step):
                ring(mat, way, step, half).wait_send()
        for i in range(6):
            rs_copy(mat, i).wait_send()
    for arr in range(2):
        for h in range(2):

            @pl.when(foreign(h))
            def _():
                piece(arr, h).wait_send()

        for off in range(1, NY):
            spread(arr, off).wait_send()
        for off in range(NY):
            to_sibling(arr, wrap(y - off, NY), off).wait_send()

    @pl.when(t == 0)
    def _():
        for arr in range(2):

            def one(j, carry):
                rcopy(WIN.at[arr], WIN.at[arr], ws.at[arr], wr.at[arr], (dp, j)).wait_send()
                return carry

            lax.fori_loop(1, NT, one, 0)

    for i in range(4):
        h_copy(i).wait_send()
    pair_copy.wait_send()
    drain(PS.at[pl.ds(0, NY - 1)], ry_s.at[0])
    for i in range(2):

        @pl.when(foreign(i))
        def _():
            rcopy(FY.at[i], FY.at[i], fs.at[i], fr.at[i], (dp, t)).wait_send()

    for k in range(2):

        @pl.when(dp < 28)
        def _():
            drain(P28.at[k, pl.ds(0, 27)], cs.at[k, 0])
            drain(R28.at[k, pl.ds(0, 31)], cs.at[k, 1])

        @pl.when(dp >= 28)
        def _():
            drain(P28.at[k, pl.ds(0, 28)], cs.at[k, 0])

        @pl.when(t < 8)
        def _():
            drain(P8.at[k, pl.ds(0, 7)], cs.at[k, 2])
            drain(R8D.at[k, pl.ds(0, 31)], cs.at[k, 3])
            drain(R8T.at[k, pl.ds(0, 15)], cs.at[k, 4])

        @pl.when(t >= 8)
        def _():
            drain(P8.at[k, pl.ds(0, 8)], cs.at[k, 2])

    drain(GR.at[pl.ds(0, NT - 1)], gs.at[0])
    store_u.wait()
    store_d.wait()


def shards(tokens, out_grad, up_weight, down_weight, up_accum, down_accum, up_q, down_q):
    rows, feats = tokens.shape
    hid = up_weight.shape[1]
    win = up_accum.shape[1]
    rank = up_q.shape[1]
    quarter = NZ * 128
    vmem = pl.BlockSpec(memory_space=pltpu.VMEM)
    hbm = pl.BlockSpec(memory_space=pl.ANY)
    sem = pltpu.SemaphoreType.DMA
    V = pltpu.VMEM
    shape = jax.ShapeDtypeStruct
    outs = pl.pallas_call(
        kernel,
        out_shape=[
            shape((rows, feats), BF16),
            shape((win, rank), F32),
            shape((hid, rank), F32),
            shape((hid, rank), F32),
            shape((win, rank), F32),
            shape(up_accum.shape, F32),
            shape(down_accum.shape, F32),
        ],
        in_specs=[vmem] * 6 + [hbm] * 2,
        out_specs=[vmem] * 5 + [hbm] * 2,
        scratch_shapes=[
            V((2, NX, rows, quarter), BF16),
            V((NZ, 128, hid), BF16),
            V((hid, quarter), BF16),
            V((2, rows, win), BF16),
            V((2, NX, rows, hid), F32),
            V((2, 3, rows, hid), BF16),
            V((2, 2, rows // 2, hid), BF16),
            V((2, 2, rows, hid), BF16),
            V((NX, rows, hid), BF16),
            V((NX, rows, quarter), BF16),
            V((2, rows, quarter), BF16),
            V((NY, 2, rows, 128), BF16),
            V((NY, 2, rows, 128), BF16),
            V((2, rows, 128), BF16),
            V((2, rows, 128), BF16),
            V((win, hid), F32),
            V((hid, win), F32),
            V((2, 28, 8, 128), F32),
            V((2, NDP, 8, 128), F32),
            V((2, 28, 8, 128), F32),
            V((2, 8, 8, 128), F32),
            V((2, NT, 8, 128), F32),
            V((2, NDP, 8, 128), F32),
            V((2, 8, 8, 128), F32),
            V((NT, 8, 128), F32),
            sem((2,)),
            sem((2,)),
            sem((2, 2, 2, 4)),
            sem((2, 2, 2, 4)),
            sem((2, 2)),
            sem((2, 2)),
            sem((2, NY)),
            sem((2, NY)),
            sem((2, NY)),
            sem((2, NY)),
            sem((2,)),
            sem((2,)),
            sem((2, 6)),
            sem((2, 6)),
            sem((4,)),
            sem((4,)),
            sem((1,)),
            sem((1,)),
            sem((1,)),
            sem((1,)),
            sem((2,)),
            sem((2,)),
            sem((2, 5)),
            sem((2, 5)),
            sem((1,)),
            sem((1,)),
        ],
        compiler_params=pltpu.CompilerParams(
            collective_id=0, has_side_effects=True, vmem_limit_bytes=56 * 1024 * 1024
        ),
    )(tokens, out_grad, up_weight, down_weight, up_q, down_q, up_accum, down_accum)
    input_grad, up_left, up_right, down_left, down_right, up_error, down_error = outs
    return input_grad, up_error, up_left, up_right, down_error, down_left, down_right


def solution(mesh):
    return jax.shard_map(
        shards,
        mesh=mesh,
        in_specs=(
            P("dp", "tensor"),
            P("dp", "tensor"),
            P("dp", "tensor"),
            P("tensor", "dp"),
            P("dp", None, "tensor"),
            P("dp", "tensor", None),
            P("tensor", None),
            P(),
        ),
        out_specs=(
            P("dp", "tensor"),
            P("dp", None, "tensor"),
            P(),
            P("tensor", None),
            P("dp", "tensor", None),
            P("tensor", None),
            P(),
        ),
        check_vma=False,
    )
```

time: 463 us -> 132 us (0.29)
  waiting for transfers between devices: 265 us -> 0 us
  Pallas kernels: 0 us -> 118 us
  blocking collectives: 62.2 us -> 0 us
  starting transfers between devices: 57.2 us -> 0 us
  matrix products: 28.4 us -> 0 us
  other arithmetic: 17.8 us -> 0 us
  between operations: 14.2 us -> 0.66 us
  local copies, waits for them, and re-layouts: 17.4 us -> 12.6 us
    all_gather x3 -> x0, waiting for transfers between devices: 194 us -> none  [the longest x2 172 us: gather_axes(): filled = lax.all_gather(filled, axes[number], axis=dim, tiled=True)]
    pallas_call x0 -> x1, Pallas kernels: none -> 118 us  [shards(): pl.pallas_call(kernel, out_shape=[shape((rows, feats), BF16), shape((win,...]
    all_to_all x10 -> x0, waiting for transfers between devices: 70.7 us -> none  [the longest x5 38.7 us: summed_on_arrival(): lax.all_to_all(pieces, axis, split_axis=0, concat_axis=0, tiled=True)]
    all_gather x4 -> x0, blocking collectives: 62.2 us -> none  [the longest x2 33.8 us: over_pieces(): return lax.all_gather(shard, axis).astype(jnp.float32).sum(0)]
    all_to_all x10 -> x0, starting transfers between devices: 57 us -> none  [the longest x5 31.4 us: summed_on_arrival(): lax.all_to_all(pieces, axis, split_axis=0, concat_axis=0, tiled=True)]
    dot_general x13 -> x0, matrix products: 27.7 us -> none  [the longest x2 11.4 us: contract_last(): lax.dot_general(left_arr, right_arr, (((1,), (1,)), ((), ())), preferred_...]
    another operation x10 -> x0, other arithmetic: 13.4 us -> none  [the longest x6 7.19 us: solve_rows(): lower_factor = jnp.linalg.cholesky(gram)]
    unnamed x34 -> x17, local copies, waits for them, and re-layouts: 10.7 us -> 12.6 us
  transfers between devices with their start and end apart: 13 -> 0, of which waited for: 12 -> 0; matrix products, arithmetic and copies ran while one was open for 9% -> 0% of each run, Pallas kernels for 0% -> 0%
where the time goes in v1:
time: 132 us; the launch traced here: 131 us
  Pallas kernels  118 us (89%)
  local copies, waits for them, and re-layouts  12.6 us (10%)
    pallas_call x1, Pallas kernels, shards(): pl.pallas_call(kernel, out_shape=[shape((rows, feats), BF16), shape((win,...  118 us
    unnamed x17, local copies, waits for them, and re-layouts  12.6 us

profile of v1, /device:TPU:1, one launch (start us, length us, event | category | flops | bytes accessed | tf_op | source)
XLA Modules:
  0.0 131.3 jit_solution(7494374030949337500)
XLA Ops:
  0.6 0.0 copy-start.2
  0.6 1.5 %copy.16.dq = f32[256,32]{1,0:T(8,128)} copy(f32[256,32]{0,1:T(8,128)} %param.15) | data formatting | bytes 65536 | tf_op args[7]
  2.2 0.0 copy-done.2
  2.2 1.0 copy.15.uq
  3.2 118.0 %shard_map.135 = (bf16[128,256]{1,0:T(8,128)(2,1)}, f32[256,32]{1,0:T(8,128)}, f32[896,32]{1,0:T(8,128)}, f32[896,32]{1,0:T(8,128)}, f32[256,32]{1,0:T(8,128)}, ...) custom-call(bf16[128,256]{1,0:T(8,128)(2,1)} %tok.1, bf16[128,256]{1,0:T(8,128)(2,1)} %og.1, bf16[128,896]{1,0:T(8,128)(2,1)} %wu.1, ...), custom_call_target="tpu_custom_call" | custom-call | tf_op jit(solution)/shard_map/pallas_call | solution.py:638
  121.2 0.0 copy-start.1
  121.2 1.7 %copy.17 = f32[256,32]{0,1:T(8,128)} copy(f32[256,32]{1,0:T(8,128)} %get-tuple-element.23) | data formatting | bytes 65536
  122.9 1.6 %copy.20 = f32[256,32]{0,1:T(8,128)} copy(f32[256,32]{1,0:T(8,128)} %get-tuple-element.27) | data formatting | bytes 65536
  124.5 1.8 %copy.18 = f32[896,32]{0,1:T(8,128)} copy(f32[896,32]{1,0:T(8,128)} %get-tuple-element.24) | data formatting | bytes 229376
  126.3 0.0 copy-start.3
  126.3 1.9 %copy.19 = f32[896,32]{0,1:T(8,128)} copy(f32[896,32]{1,0:T(8,128)} %get-tuple-element.26) | data formatting | bytes 229376
  128.2 0.0 copy-done.3
  128.2 0.6 copy.24
  128.8 0.0 copy-done.1
  128.8 0.0 copy-start
  128.8 0.9 copy.25
  129.7 0.6 copy-done
  130.3 0.9 copy.26
Async XLA Ops:
  0.6 1.6 %copy-start.2 = (f32[896,32]{0,1:T(8,128)S(1)}, f32[896,32]{0,1:T(8,128)}, u32[]{:S(2)}) copy-start(f32[896,32]{0,1:T(8,128)} %param.14) | copy-start | bytes 344068
  121.2 7.6 %copy-start.1 = (f32[1,256,896]{2,1,0:T(8,128)S(1)}, f32[1,256,896]{2,1,0:T(8,128)}, u32[]{:S(2)}) copy-start(f32[1,256,896]{2,1,0:T(8,128)} %get-tuple-element.36) | copy-start | bytes 2752516
  126.3 1.9 %copy-start.3 = (bf16[128,256]{1,0:T(8,128)(2,1)S(1)}, bf16[128,256]{1,0:T(8,128)(2,1)}, u32[]{:S(2)}) copy-start(bf16[128,256]{1,0:T(8,128)(2,1)} %get-tuple-element.35) | copy-start | bytes 196612
  128.8 1.5 %copy-start = (f32[1,896,256]{2,1,0:T(8,128)S(1)}, f32[1,896,256]{2,1,0:T(8,128)}, u32[]{:S(2)}) copy-start(f32[1,896,256]{2,1,0:T(8,128)} %get-tuple-element.39) | copy-start | bytes 2752516

commit v2 on v1

--- a/solution.py
+++ b/solution.py
@@ -43,12 +43,16 @@
     return work[:, n : 2 * n]
 
 
+GROUPS = ((0, 512), (512, 384))
+
+
 def kernel(
-    tok, og, wu, wd, uq, dq, uacc, dacc,
-    ig_out, ul_out, ur_out, dl_out, dr_out, uerr, derr,
+    tok_in, og_in, wu_in, wd_in, uq_in, dq_in, uacc, dacc,
+    ig_out, ul_out, ur_out, dl_out, dr_out, mu_out, md_out,
+    TO, UQ, DQ, AU, AD, GQ, UL, UR, DL, DR,
     A, WU, WD, WIN, PF, SB, FB, RB, HG, IGP, IGX, PS, RY, FY, IGO, MU, MD,
     P28, R28, L28, P8, R8T, R8D, L8, GR,
-    acc_sem, err_sem, ring_s, ring_r, xs, xr, ys, yr, ds, dr, ws, wr,
+    in_sem, acc_sem, out_sem, ring_s, ring_r, xs, xr, ys, yr, ds, dr, ws, wr,
     rs_s, rs_r, hs, hr, ps_s, ps_r, ry_s, ry_r, fs, fr, cs, cr, gs, gr,
 ):
     dp, t = lax.axis_index("dp"), lax.axis_index("tensor")
@@ -57,7 +61,8 @@
     mine = x // 2 == c
     xl, xrr = wrap(x - 1, NX), wrap(x + 1, NX)
     sib = (dp, t + 1 - 2 * c)
-    tokens = tok.shape[0]
+    tok, og = TO.at[0], TO.at[1]
+    tokens = TO.shape[1]
     grad_scale = 1.0 / math.sqrt(tokens)
 
     def lanes_of(i):
@@ -74,24 +79,25 @@
     def at_x(xi):
         return (z * NX + xi, t)
 
+    loads = [
+        pltpu.make_async_copy(src, dst, in_sem.at[i])
+        for i, (src, dst) in enumerate(
+            (
+                (wu_in, WU.at[z]),
+                (wd_in, WD.at[:, lanes_of(z)]),
+                (tok_in, tok),
+                (og_in, og),
+                (uq_in, UQ),
+                (dq_in, DQ),
+            )
+        )
+    ]
     load_u = pltpu.make_async_copy(uacc.at[0], MU, acc_sem.at[0])
     load_d = pltpu.make_async_copy(dacc.at[0], MD, acc_sem.at[1])
+    for load in loads:
+        load.start()
     load_u.start()
     load_d.start()
-
-    WU[z] = wu[...]
-    WD[:, lanes_of(z)] = wd[...]
-    for h in range(2):
-
-        @pl.when(jnp.logical_and(mine, lax.rem(x, 2) == h))
-        def _():
-            A[0, x, :, lanes_of(y)] = tok[:, h * 128 : (h + 1) * 128]
-            A[1, x, :, lanes_of(y)] = og[:, h * 128 : (h + 1) * 128]
-
-    @pl.when(t == 0)
-    def _():
-        WIN[0] = tok[...]
-        WIN[1] = og[...]
 
     barrier = pltpu.get_barrier_semaphore()
 
@@ -124,54 +130,63 @@
 
     pl.semaphore_wait(barrier, NDP + NT - 2 + 2 * jnp.where(mine, 0, 1).astype(jnp.int32))
 
-    def slot(mat, zi, half):
+    for load in loads[:4]:
+        load.wait()
+    for h in range(2):
+
+        @pl.when(jnp.logical_and(mine, lax.rem(x, 2) == h))
+        def _():
+            for arr in range(2):
+                A[arr, x, :, lanes_of(y)] = TO[arr, :, h * 128 : (h + 1) * 128]
+
+    @pl.when(t == 0)
+    def _():
+        WIN[...] = TO[...]
+
+    def slot(mat, zi, g):
+        hidden_range = pl.ds(*GROUPS[g])
         if mat == 0:
-            return WU.at[zi, pl.ds(half * 64, 64)]
-        return WD.at[pl.ds(half * 448, 448), lanes_of(zi)]
-
-    def ring(mat, way, step, half):
+            return WU.at[zi, :, hidden_range]
+        return WD.at[hidden_range, lanes_of(zi)]
+
+    def ring(mat, way, step, g):
         if way == 0:
             zi, to = wrap(z - step + 1, NZ), wrap(z + 1, NZ)
         else:
             zi, to = wrap(z + step - 1, NZ), wrap(z - 1, NZ)
-        src = slot(mat, zi, half)
-        if step == 1:
-            src = wu.at[pl.ds(half * 64, 64)] if mat == 0 else wd.at[pl.ds(half * 448, 448)]
-        i = (mat, way, half, step - 1)
-        return rcopy(src, slot(mat, zi, half), ring_s.at[i], ring_r.at[i], (to * NX + x, t))
-
-    def ring_arrived(mat, way, step, half):
+        i = (mat, way, g, step - 1)
+        ref = slot(mat, zi, g)
+        return rcopy(ref, ref, ring_s.at[i], ring_r.at[i], (to * NX + x, t))
+
+    def ring_ways(step, g):
+        return (0, 1) if step < 4 else (g,)
+
+    def ring_send(mat, step, g):
+        for way in ring_ways(step, g):
+            ring(mat, way, step, g).start()
+
+    def ring_arrived(mat, way, step, g):
         zi = wrap(z - step, NZ) if way == 0 else wrap(z + step, NZ)
-        ref = slot(mat, zi, half)
-        i = (mat, way, half, step - 1)
+        ref = slot(mat, zi, g)
+        i = (mat, way, g, step - 1)
         rcopy(ref, ref, ring_s.at[i], ring_r.at[i], (dp, t)).wait_recv()
 
-    def ring_parts(step):
-        if step < 4:
-            return [(way, half) for half in range(2) for way in range(2)]
-        return [(0, 0), (1, 1)]
-
-    def ring_send(mat, step, halves=(0, 1)):
-        for way, half in ring_parts(step):
-            if half in halves:
-                ring(mat, way, step, half).start()
-
-    def ring_pass(mat, step):
-        nxt = ring_parts(step)
-        for way, half in ring_parts(step - 1):
-            ring_arrived(mat, way, step - 1, half)
-            if (way, half) in nxt:
-                ring(mat, way, step, half).start()
-
-    def ring_end(mat):
-        for way, half in ring_parts(4):
-            ring_arrived(mat, way, 4, half)
-
-    ring_send(0, 1)
+    def ring_pass(mat, step, g):
+        for way in ring_ways(step - 1, g):
+            ring_arrived(mat, way, step - 1, g)
+            if way in ring_ways(step, g):
+                ring(mat, way, step, g).start()
+
+    def ring_end(mat, g):
+        for way in ring_ways(4, g):
+            ring_arrived(mat, way, 4, g)
+
+    ring_send(0, 1, 0)
+    ring_send(1, 1, 0)
 
     def piece(arr, h):
         xd = 2 * c + h
-        src = (tok, og)[arr].at[:, pl.ds(h * 128, 128)]
+        src = TO.at[arr, :, pl.ds(h * 128, 128)]
         return rcopy(
             src,
             A.at[arr, x, :, lanes_of(y)],
@@ -200,7 +215,6 @@
     def to_sibling(arr, yi, off):
         return rcopy(pair(arr, yi), pair(arr, yi), ds.at[arr, off], dr.at[arr, off], sib)
 
-    ring_send(1, 1, (0,))
     for arr in range(2):
         for h in range(2):
 
@@ -235,23 +249,16 @@
             ref = A.at[arr, pl.ds(2 - 2 * c, 2), :, lanes_of(yi)]
             rcopy(ref, ref, ds.at[arr, off], dr.at[arr, off], (dp, t)).wait_recv()
 
-    ring_pass(0, 2)
-    ring_send(1, 1, (1,))
-    ring_pass(0, 3)
-    ring_pass(1, 2)
-    ring_pass(0, 4)
-    y_arrivals(0)
-    ring_pass(1, 3)
-    sibling_arrivals(0)
-    ring_end(0)
-
-    def products(mat):
+    def products(mat, g):
+        lo, size = GROUPS[g]
+        cols = slice(lo, lo + size)
+
         def one(d, carry):
             xi = wrap(x + d, NX)
             if mat == 0:
-                PF[0, d] = dot_nn(A[0, xi], WU[...].reshape(NZ * 128, WU.shape[2]))
+                PF[0, d, :, cols] = dot_nn(A[0, xi], WU[:, :, cols].reshape(NZ * 128, size))
             else:
-                PF[1, d] = dot_nt(A[1, xi], WD[...])
+                PF[1, d, :, cols] = dot_nt(A[1, xi], WD[cols, :])
             return carry
 
         lax.fori_loop(0, NX, one, 0)
@@ -259,55 +266,93 @@
     half_rows = tokens // 2
     top, bot = pl.ds(0, half_rows), pl.ds(half_rows, half_rows)
 
-    def rs_copy(mat, i):
-        src = (SB.at[mat, 1, top], SB.at[mat, 1, bot], SB.at[mat, 0, bot],
-               SB.at[mat, 2, top], SB.at[mat, 0, top], SB.at[mat, 2, bot])[i]
-        dst = (FB.at[mat, 0], FB.at[mat, 1], RB.at[mat, 0, bot],
-               RB.at[mat, 1, top], RB.at[mat, 0, top], RB.at[mat, 1, bot])[i]
+    def rs_copy(mat, g, i):
+        cols = pl.ds(*GROUPS[g])
+        src = (SB.at[mat, 1, top, cols], SB.at[mat, 1, bot, cols], SB.at[mat, 0, bot, cols],
+               SB.at[mat, 2, top, cols], SB.at[mat, 0, top, cols], SB.at[mat, 2, bot, cols])[i]
+        dst = (FB.at[mat, 0, :, cols], FB.at[mat, 1, :, cols], RB.at[mat, 0, bot, cols],
+               RB.at[mat, 1, top, cols], RB.at[mat, 0, top, cols], RB.at[mat, 1, bot, cols])[i]
         to = at_x(xrr if i % 2 == 0 else xl)
-        return rcopy(src, dst, rs_s.at[mat, i], rs_r.at[mat, i], to)
-
-    def rs_first(mat):
-        SB[mat, 1] = PF[mat, 2].astype(BF16)
-        rs_copy(mat, 0).start()
-        rs_copy(mat, 1).start()
-        SB[mat, 0, half_rows:] = PF[mat, 1, half_rows:].astype(BF16)
-        rs_copy(mat, 2).start()
-        SB[mat, 2, :half_rows] = PF[mat, 3, :half_rows].astype(BF16)
-        rs_copy(mat, 3).start()
-
-    def rs_second(mat):
-        rs_copy(mat, 0).wait_recv()
-        SB[mat, 0, :half_rows] = (PF[mat, 1, :half_rows] + FB[mat, 0].astype(F32)).astype(BF16)
-        rs_copy(mat, 4).start()
-        rs_copy(mat, 1).wait_recv()
-        SB[mat, 2, half_rows:] = (PF[mat, 3, half_rows:] + FB[mat, 1].astype(F32)).astype(BF16)
-        rs_copy(mat, 5).start()
-
-    def rs_end(mat):
+        return rcopy(src, dst, rs_s.at[mat, g, i], rs_r.at[mat, g, i], to)
+
+    def rs_first(mat, g):
+        cols = slice(GROUPS[g][0], sum(GROUPS[g]))
+        SB[mat, 1, :, cols] = PF[mat, 2, :, cols].astype(BF16)
+        rs_copy(mat, g, 0).start()
+        rs_copy(mat, g, 1).start()
+        SB[mat, 0, half_rows:, cols] = PF[mat, 1, half_rows:, cols].astype(BF16)
+        rs_copy(mat, g, 2).start()
+        SB[mat, 2, :half_rows, cols] = PF[mat, 3, :half_rows, cols].astype(BF16)
+        rs_copy(mat, g, 3).start()
+
+    def rs_second(mat, g):
+        cols = slice(GROUPS[g][0], sum(GROUPS[g]))
+        rs_copy(mat, g, 0).wait_recv()
+        SB[mat, 0, :half_rows, cols] = (
+            PF[mat, 1, :half_rows, cols] + FB[mat, 0, :, cols].astype(F32)
+        ).astype(BF16)
+        rs_copy(mat, g, 4).start()
+        rs_copy(mat, g, 1).wait_recv()
+        SB[mat, 2, half_rows:, cols] = (
+            PF[mat, 3, half_rows:, cols] + FB[mat, 1, :, cols].astype(F32)
+        ).astype(BF16)
+        rs_copy(mat, g, 5).start()
+
+    def rs_end(mat, g):
         for i in range(2, 6):
-            rs_copy(mat, i).wait_recv()
-
-    products(0)
-    rs_first(0)
+            rs_copy(mat, g, i).wait_recv()
+
+    ring_pass(0, 2, 0)
+    ring_pass(1, 2, 0)
+    loads[4].wait()
+    load_u.wait()
+    AU[...] = dot_nt(UQ[...], MU[...], HI)
+    ring_pass(0, 3, 0)
+    ring_pass(1, 3, 0)
+    ring_send(0, 1, 1)
+    loads[5].wait()
+    load_d.wait()
+    AD[...] = dot_nt(DQ[...], MD[...], HI)
+    ring_pass(0, 4, 0)
+    ring_pass(1, 4, 0)
+    ring_send(1, 1, 1)
+    y_arrivals(0)
+    ring_pass(0, 2, 1)
+    ring_end(0, 0)
+    sibling_arrivals(0)
+    products(0, 0)
+    rs_first(0, 0)
+    ring_pass(1, 2, 1)
     y_arrivals(1)
-    ring_pass(1, 4)
-    rs_second(0)
+    ring_pass(0, 3, 1)
+    ring_end(1, 0)
     sibling_arrivals(1)
-    ring_end(1)
-    products(1)
-    rs_first(1)
-    rs_end(0)
-    load_u.wait()
-    load_d.wait()
+    products(1, 0)
+    rs_first(1, 0)
+    rs_second(0, 0)
+    ring_pass(1, 3, 1)
+    rs_second(1, 0)
 
     @pl.when(t != 0)
     def _():
         for arr in range(2):
             rcopy(WIN.at[arr], WIN.at[arr], ws.at[arr], wr.at[arr], (dp, t)).wait_recv()
 
-    rs_second(1)
-    rs_end(1)
+    ring_pass(0, 4, 1)
+    ring_pass(1, 4, 1)
+    GQ[...] = dot_nt(DQ[...], WIN[1].astype(F32), HI)
+    rs_end(0, 0)
+    ring_end(0, 1)
+    products(0, 1)
+    rs_first(0, 1)
+    ring_end(1, 1)
+    products(1, 1)
+    rs_first(1, 1)
+    rs_second(0, 1)
+    rs_end(1, 0)
+    rs_end(0, 1)
+    rs_second(1, 1)
+    rs_end(1, 1)
     preact = PF[0, 0] + RB[0, 0].astype(F32) + RB[0, 1].astype(F32)
     back = PF[1, 0] + RB[1, 0].astype(F32) + RB[1, 1].astype(F32)
     squash = jax.nn.sigmoid(preact)
@@ -315,9 +360,6 @@
     hidden = (back * squash * (1.0 + preact * (1.0 - squash))).astype(BF16)
     HG[x] = hidden
 
-    MU[...] += dot_nn(WIN[0].T, hidden) * grad_scale
-    MD[...] += dot_nn(act.T, WIN[1]) * grad_scale
-
     def put28(k, arr):
         for g in range(4):
             for l in range(7):
@@ -425,9 +467,10 @@
         def _():
             drain(L8.at[k, pl.ds(0, 8)], cr.at[k, 4])
 
-    put8(0, dot_nn(MU[...], uq[...], HI).T)
+    hq = dot_nt(UQ[...], hidden.astype(F32), HI)
+    put8(0, AU[...] + dot_nn(hq, WIN[0].astype(F32), HI) * grad_scale)
     send8(0)
-    put28(0, dot_nn(MD[...], dq[...], HI).T)
+    put28(0, AD[...] + dot_nn(GQ[...], act.astype(F32), HI) * grad_scale)
     send28(0)
 
     def h_copy(i):
@@ -440,15 +483,36 @@
         ref = (HG.at[xl], HG.at[xrr], HG.at[x2, top], HG.at[x2, bot])[i]
         rcopy(ref, ref, hs.at[i], hr.at[i], (dp, t)).wait_recv()
 
+    def ig_product(i):
+        IGP[i] = dot_nt(HG[i], WU[...].reshape(NZ * 128, WU.shape[2])).astype(BF16)
+
     h_copy(0).start()
     h_copy(1).start()
+    MU[...] += dot_nn(WIN[0].T, hidden) * grad_scale
+    MD[...] += dot_nn(act.T, WIN[1]) * grad_scale
+    store_u = pltpu.make_async_copy(MU, mu_out, acc_sem.at[0])
+    store_d = pltpu.make_async_copy(MD, md_out, acc_sem.at[1])
+    store_u.start()
+    store_d.start()
     middle8(0)
     reduce28(0)
     h_wait(0)
     h_copy(2).start()
     h_wait(1)
     h_copy(3).start()
+
+    def ig_near(d, carry):
+        ig_product(wrap(x + d - 1, NX))
+        return carry
+
+    lax.fori_loop(0, 3, ig_near, 0)
     reduce8(0)
+    h_wait(2)
+    h_wait(3)
+    lax.fori_loop(3, 4, ig_near, 0)
+    other = IGP.at[pl.ds(2 - 2 * c, 2)]
+    pair_copy = rcopy(other, IGX, ps_s.at[0], ps_r.at[0], sib)
+    pair_copy.start()
 
     end28(0)
     down_sum = get(L28, 0, 7)
@@ -466,30 +530,6 @@
 
     lax.fori_loop(0, NT, gram_send, 0)
 
-    end8(0)
-    up_sum = get(L8, 0, 2)
-    put28(1, dot_nn(up_sum, MU[...], HI))
-    send28(1)
-
-    h_wait(2)
-    h_wait(3)
-
-    def ig_one(i, carry):
-        IGP[i] = dot_nt(HG[i], WU[...].reshape(NZ * 128, WU.shape[2])).astype(BF16)
-        return carry
-
-    lax.fori_loop(0, NX, ig_one, 0)
-    other = IGP.at[pl.ds(2 - 2 * c, 2)]
-    pair_copy = rcopy(other, IGX, ps_s.at[0], ps_r.at[0], sib)
-    pair_copy.start()
-
-    middle8(1)
-    up_inv = inverse_factor(dot_nt(up_sum, up_sum, HI))
-    up_left_t = dot_nn(up_inv, up_sum, HI)
-    up_left = up_left_t.T
-    ul_out[...] = up_left
-    reduce28(1)
-
     pair_copy.wait_recv()
     for i in range(2):
         both = (IGP[2 * c + i].astype(F32) + IGX[i].astype(F32)).astype(BF16)
@@ -497,36 +537,35 @@
             PS[k, i] = both[:, k * 128 : (k + 1) * 128]
     RY[y] = PS[y]
 
-    def ry_send(j, carry):
-        @pl.when(j != y)
-        def _():
-            rcopy(PS.at[j], RY.at[y], ry_s.at[0], ry_r.at[0], (dp, 2 * j + c)).start()
-
+    def ry_send(off, carry):
+        j = wrap(y + off, NY)
+        rcopy(PS.at[j], RY.at[y], ry_s.at[0], ry_r.at[0], (dp, 2 * j + c)).start()
         return carry
 
-    lax.fori_loop(0, NY, ry_send, 0)
-
-    reduce8(1)
+    lax.fori_loop(1, NY, ry_send, 0)
+
+    end8(0)
+    up_sum = get(L8, 0, 2)
+    put28(1, dot_nn(up_sum, MU[...], HI))
+    send28(1)
+    middle8(1)
+
+    def put_out(ref, value, dst, i):
+        ref[...] = value
+        copy = pltpu.make_async_copy(ref, dst, out_sem.at[i])
+        copy.start()
+        return copy
+
+    results = []
+    up_inv = inverse_factor(dot_nt(up_sum, up_sum, HI))
+    results.append(put_out(UL, dot_nn(up_inv, up_sum, HI), ul_out, 0))
+    reduce28(1)
     drain(GR.at[pl.ds(0, NT - 1)], gr.at[0])
     packed = jnp.sum(GR[...], axis=0)
     gram = jnp.concatenate([packed[:, 32 * g : 32 * g + 32] for g in range(4)], axis=0)
+    reduce8(1)
     down_inv = inverse_factor(gram)
-    down_left = dot_nn(down_inv, down_sum, HI).T
-    dl_out[...] = down_left
-
-    end28(1)
-    up_right_t = dot_nn(up_inv, get(L28, 1, 7), HI) * (1.0 / NDP)
-    ur_out[...] = up_right_t.T
-    MU[...] -= dot_nn(up_left, up_right_t, HI)
-    store_u = pltpu.make_async_copy(MU, uerr.at[0], err_sem.at[0])
-    store_u.start()
-
-    end8(1)
-    down_right_t = dot_nn(down_inv, get(L8, 1, 2), HI) * (1.0 / NDP)
-    dr_out[...] = down_right_t.T
-    MD[...] -= dot_nn(down_left, down_right_t, HI)
-    store_d = pltpu.make_async_copy(MD, derr.at[0], err_sem.at[1])
-    store_d.start()
+    results.append(put_out(DL, dot_nn(down_inv, down_sum, HI), dl_out, 1))
 
     drain(RY.at[pl.ds(0, NY - 1)], ry_r.at[0])
     for i in range(2):
@@ -552,20 +591,33 @@
         def _():
             IGO[h] = FY[h]
 
+    end28(1)
+    results.append(
+        put_out(UR, dot_nn(up_inv, get(L28, 1, 7), HI) * (1.0 / NDP), ur_out, 2)
+    )
     for h in range(2):
 
         @pl.when(foreign(h))
         def _():
             rcopy(IGO.at[h], IGO.at[h], fs.at[h], fr.at[h], (dp, t)).wait_recv()
 
-        ig_out[:, h * 128 : (h + 1) * 128] = IGO[h]
+        copy = pltpu.make_async_copy(
+            IGO.at[h], ig_out.at[:, pl.ds(h * 128, 128)], out_sem.at[4 + h]
+        )
+        copy.start()
+        results.append(copy)
+    end8(1)
+    results.append(
+        put_out(DR, dot_nn(down_inv, get(L8, 1, 2), HI) * (1.0 / NDP), dr_out, 3)
+    )
 
     for mat in range(2):
-        for step in range(1, 5):
-            for way, half in ring_parts(step):
-                ring(mat, way, step, half).wait_send()
-        for i in range(6):
-            rs_copy(mat, i).wait_send()
+        for g in range(2):
+            for step in range(1, 5):
+                for way in ring_ways(step, g):
+                    ring(mat, way, step, g).wait_send()
+            for i in range(6):
+                rs_copy(mat, g, i).wait_send()
     for arr in range(2):
         for h in range(2):
 
@@ -622,6 +674,28 @@
     drain(GR.at[pl.ds(0, NT - 1)], gs.at[0])
     store_u.wait()
     store_d.wait()
+    for copy in results:
+        copy.wait()
+
+
+def finish(*refs):
+    ins, outs, held = refs[:7], refs[7:14], refs[14:21]
+    came, left = refs[21], refs[22]
+    loads = [pltpu.make_async_copy(ins[i], held[i], came.at[i]) for i in range(7)]
+    ends = [outs[i] if i < 5 else outs[i].at[0] for i in range(7)]
+    stores = [pltpu.make_async_copy(held[i], ends[i], left.at[i]) for i in range(7)]
+    for i in (1, 2, 5, 3, 4, 6, 0):
+        loads[i].start()
+    for i, low, high in ((5, 1, 2), (6, 3, 4)):
+        for k in (low, high, i):
+            loads[k].wait()
+        held[i][...] -= dot_nn(held[low][...].T, held[high][...], HI)
+        for k in (i, low, high):
+            stores[k].start()
+    loads[0].wait()
+    stores[0].start()
+    for store in stores:
+        store.wait()
 
 
 def shards(tokens, out_grad, up_weight, down_weight, up_accum, down_accum, up_q, down_q):
@@ -630,7 +704,6 @@
     win = up_accum.shape[1]
     rank = up_q.shape[1]
     quarter = NZ * 128
-    vmem = pl.BlockSpec(memory_space=pltpu.VMEM)
     hbm = pl.BlockSpec(memory_space=pl.ANY)
     sem = pltpu.SemaphoreType.DMA
     V = pltpu.VMEM
@@ -639,16 +712,26 @@
         kernel,
         out_shape=[
             shape((rows, feats), BF16),
-            shape((win, rank), F32),
-            shape((hid, rank), F32),
-            shape((hid, rank), F32),
-            shape((win, rank), F32),
-            shape(up_accum.shape, F32),
-            shape(down_accum.shape, F32),
+            shape((rank, win), F32),
+            shape((rank, hid), F32),
+            shape((rank, hid), F32),
+            shape((rank, win), F32),
+            shape((win, hid), F32),
+            shape((hid, win), F32),
         ],
-        in_specs=[vmem] * 6 + [hbm] * 2,
-        out_specs=[vmem] * 5 + [hbm] * 2,
+        in_specs=[hbm] * 8,
+        out_specs=[hbm] * 7,
         scratch_shapes=[
+            V((2, rows, feats), BF16),
+            V((rank, hid), F32),
+            V((rank, win), F32),
+            V((rank, win), F32),
+            V((rank, hid), F32),
+            V((rank, rows), F32),
+            V((rank, win), F32),
+            V((rank, hid), F32),
+            V((rank, hid), F32),
+            V((rank, win), F32),
             V((2, NX, rows, quarter), BF16),
             V((NZ, 128, hid), BF16),
             V((hid, quarter), BF16),
@@ -674,8 +757,9 @@
             V((2, NDP, 8, 128), F32),
             V((2, 8, 8, 128), F32),
             V((NT, 8, 128), F32),
+            sem((6,)),
             sem((2,)),
-            sem((2,)),
+            sem((6,)),
             sem((2, 2, 2, 4)),
             sem((2, 2, 2, 4)),
             sem((2, 2)),
@@ -686,8 +770,8 @@
             sem((2, NY)),
             sem((2,)),
             sem((2,)),
-            sem((2, 6)),
-            sem((2, 6)),
+            sem((2, 2, 6)),
+            sem((2, 2, 6)),
             sem((4,)),
             sem((4,)),
             sem((1,)),
@@ -702,11 +786,38 @@
             sem((1,)),
         ],
         compiler_params=pltpu.CompilerParams(
-            collective_id=0, has_side_effects=True, vmem_limit_bytes=56 * 1024 * 1024
+            collective_id=0, has_side_effects=True, vmem_limit_bytes=63 * 1024 * 1024
         ),
-    )(tokens, out_grad, up_weight, down_weight, up_q, down_q, up_accum, down_accum)
-    input_grad, up_left, up_right, down_left, down_right, up_error, down_error = outs
-    return input_grad, up_error, up_left, up_right, down_error, down_left, down_right
+    )(tokens, out_grad, up_weight, down_weight, up_q.T, down_q.T, up_accum, down_accum)
+    input_grad, ul, ur, dl, dr, mu, md = outs
+    results = pl.pallas_call(
+        finish,
+        out_shape=[
+            shape((rows, feats), BF16),
+            shape((rank, win), F32),
+            shape((rank, hid), F32),
+            shape((rank, hid), F32),
+            shape((rank, win), F32),
+            shape(up_accum.shape, F32),
+            shape(down_accum.shape, F32),
+        ],
+        in_specs=[hbm] * 7,
+        out_specs=[hbm] * 7,
+        scratch_shapes=[
+            V((rows, feats), BF16),
+            V((rank, win), F32),
+            V((rank, hid), F32),
+            V((rank, hid), F32),
+            V((rank, win), F32),
+            V((win, hid), F32),
+            V((hid, win), F32),
+            sem((7,)),
+            sem((7,)),
+        ],
+        compiler_params=pltpu.CompilerParams(vmem_limit_bytes=63 * 1024 * 1024),
+    )(input_grad, ul, ur, dl, dr, mu, md)
+    input_grad, ul, ur, dl, dr, up_error, down_error = results
+    return input_grad, up_error, ul.T, ur.T, down_error, dl.T, dr.T
 
 
 def solution(mesh):

time: 132 us -> 116 us (0.88)
  local copies, waits for them, and re-layouts: 12.6 us -> 0 us
  Pallas kernels: 118 us -> 115 us
    unnamed x17 -> x0, local copies, waits for them, and re-layouts: 12.6 us -> none
    pallas_call x1 -> x2, Pallas kernels: 118 us -> 115 us  [the longest x1 110 us: shards(): pl.pallas_call(kernel, out_shape=[shape((rows, feats), BF16), shape((rank...]
where the time goes in v2:
time: 116 us; the launch traced here: 115 us
  Pallas kernels  115 us (99%)
    pallas_call x1, Pallas kernels, shards(): pl.pallas_call(kernel, out_shape=[shape((rows, feats), BF16), shape((rank...  110 us
    pallas_call x1, Pallas kernels, shards(): pl.pallas_call(finish, out_shape=[shape((rows, feats), BF16), shape((rank...  4.41 us

profile of v2, /device:TPU:1, one launch (start us, length us, event | category | flops | bytes accessed | tf_op | source)
XLA Modules:
  0.0 115.4 jit_solution(14956299383467439226)
XLA Ops:
  0.6 110.3 %shard_map.135 = (bf16[128,256]{1,0:T(8,128)(2,1)}, f32[32,256]{1,0:T(8,128)}, f32[32,896]{1,0:T(8,128)}, f32[32,896]{1,0:T(8,128)}, f32[32,256]{1,0:T(8,128)}, /*index=5*/f32[256,896]{1,0:T(8,128)}, f32[896,256]{1,0:T(8,128)}) custom-call(bf16[128,256]{1,0:T(8,128)(2,1)} %tok_in.1, bf16[128,256]{1,0:T(8,128)(2,1)} %og_in.1, bf16[128,896]{1,0:T(8,128)(2,1)} %wu_in.1, ...), custom_call_target="tpu_custom_call" | custom-call | tf_op jit(solution)/shard_map/pallas_call | solution.py:711
  111.0 4.4 %shard_map.136 = (bf16[128,256]{1,0:T(8,128)(2,1)}, f32[32,256]{1,0:T(8,128)}, f32[32,896]{1,0:T(8,128)}, f32[32,896]{1,0:T(8,128)}, f32[32,256]{1,0:T(8,128)}, ...) custom-call(bf16[128,256]{1,0:T(8,128)(2,1)} %get-tuple-element.21.refs_0_, f32[32,256]{1,0:T(8,128)} %get-tuple-element.22.refs_1_, ...), custom_call_target="tpu_custom_call" | custom-call | tf_op jit(solution)/shard_map/pallas_call | solution.py:793

commit v3 on v2

--- a/solution.py
+++ b/solution.py
@@ -17,6 +17,21 @@
 
 def wrap(a, n):
     return lax.rem(a + 4 * n, n)
+
+
+def thirds(a):
+    high = a.astype(BF16)
+    rest = a - high.astype(F32)
+    middle = rest.astype(BF16)
+    return high, middle, (rest - middle.astype(F32)).astype(BF16)
+
+
+def dot_thirds(left_t, right_t):
+    lh, lm, ll = thirds(left_t)
+    rh, rm, rl = thirds(right_t)
+    left = jnp.concatenate([ll, lm, lh, lm, lh, lh], axis=0)
+    right = jnp.concatenate([rh, rm, rl, rh, rm, rh], axis=0)
+    return dot_nn(left.astype(F32).T.astype(BF16), right)
 
 
 def dot_nt(a, b, precision=None):
@@ -49,7 +64,7 @@
 def kernel(
     tok_in, og_in, wu_in, wd_in, uq_in, dq_in, uacc, dacc,
     ig_out, ul_out, ur_out, dl_out, dr_out, mu_out, md_out,
-    TO, UQ, DQ, AU, AD, GQ, UL, UR, DL, DR,
+    TO, ACT, UQ, DQ, AU, AD, GQ, UL, UR, DL, DR,
     A, WU, WD, WIN, PF, SB, FB, RB, HG, IGP, IGX, PS, RY, FY, IGO, MU, MD,
     P28, R28, L28, P8, R8T, R8D, L8, GR,
     in_sem, acc_sem, out_sem, ring_s, ring_r, xs, xr, ys, yr, ds, dr, ws, wr,
@@ -331,17 +346,54 @@
     rs_first(1, 0)
     rs_second(0, 0)
     ring_pass(1, 3, 1)
-    rs_second(1, 0)
+    ring_pass(0, 4, 1)
+    ring_pass(1, 4, 1)
 
     @pl.when(t != 0)
     def _():
         for arr in range(2):
             rcopy(WIN.at[arr], WIN.at[arr], ws.at[arr], wr.at[arr], (dp, t)).wait_recv()
 
-    ring_pass(0, 4, 1)
-    ring_pass(1, 4, 1)
     GQ[...] = dot_nt(DQ[...], WIN[1].astype(F32), HI)
-    rs_end(0, 0)
+    rs_second(1, 0)
+
+    def activate(g):
+        cols = slice(GROUPS[g][0], sum(GROUPS[g]))
+        preact = PF[0, 0, :, cols] + RB[0, 0, :, cols].astype(F32) + RB[0, 1, :, cols].astype(F32)
+        back = PF[1, 0, :, cols] + RB[1, 0, :, cols].astype(F32) + RB[1, 1, :, cols].astype(F32)
+        squash = jax.nn.sigmoid(preact)
+        ACT[:, cols] = (preact * squash).astype(BF16)
+        HG[x, :, cols] = (back * squash * (1.0 + preact * (1.0 - squash))).astype(BF16)
+
+    def add_up(g):
+        cols = slice(GROUPS[g][0], sum(GROUPS[g]))
+        hq = dot_nt(UQ[:, cols], HG[x, :, cols].astype(F32), HI)
+        AU[...] += dot_nn(hq, WIN[0].astype(F32), HI) * grad_scale
+
+    def add_down(g):
+        cols = slice(GROUPS[g][0], sum(GROUPS[g]))
+        AD[:, cols] += dot_nn(GQ[...], ACT[:, cols].astype(F32), HI) * grad_scale
+
+    def h_copy(g, i):
+        cols = pl.ds(*GROUPS[g])
+        own = HG.at[x, :, cols]
+        src = (own, own, HG.at[xl, top, cols], HG.at[xrr, bot, cols])[i]
+        return rcopy(src, src, hs.at[g, i], hr.at[g, i], at_x(xrr if i % 2 == 0 else xl))
+
+    def h_wait(g, i):
+        cols = pl.ds(*GROUPS[g])
+        x2 = wrap(x + 2, NX)
+        ref = (
+            HG.at[xl, :, cols], HG.at[xrr, :, cols], HG.at[x2, top, cols], HG.at[x2, bot, cols]
+        )[i]
+        rcopy(ref, ref, hs.at[g, i], hr.at[g, i], (dp, t)).wait_recv()
+
+    def h_relay(g):
+        h_wait(g, 0)
+        h_copy(g, 2).start()
+        h_wait(g, 1)
+        h_copy(g, 3).start()
+
     ring_end(0, 1)
     products(0, 1)
     rs_first(0, 1)
@@ -349,16 +401,48 @@
     products(1, 1)
     rs_first(1, 1)
     rs_second(0, 1)
+    rs_second(1, 1)
+    rs_end(0, 0)
     rs_end(1, 0)
+    activate(0)
+    h_copy(0, 0).start()
+    h_copy(0, 1).start()
+    add_up(0)
+    add_down(0)
     rs_end(0, 1)
-    rs_second(1, 1)
     rs_end(1, 1)
-    preact = PF[0, 0] + RB[0, 0].astype(F32) + RB[0, 1].astype(F32)
-    back = PF[1, 0] + RB[1, 0].astype(F32) + RB[1, 1].astype(F32)
-    squash = jax.nn.sigmoid(preact)
-    act = (preact * squash).astype(BF16)
-    hidden = (back * squash * (1.0 + preact * (1.0 - squash))).astype(BF16)
-    HG[x] = hidden
+    activate(1)
+
+    def along(at, n, visit, here):
+        visit(wrap(at + n // 2, n))
+
+        def one(i, carry):
+            visit(wrap(at + n // 2 - i, n))
+            visit(wrap(at + n // 2 + i, n))
+            return carry
+
+        lax.fori_loop(1, n // 2, one, 0)
+        here()
+
+    other_x = [wrap(x + d, NX) for d in (2, 1, 3)]
+
+    def dp_others(send):
+        def visit(zi):
+            for xi in (*other_x, x):
+                send(zi * NX + xi)
+
+        def here():
+            for xi in other_x:
+                send(z * NX + xi)
+
+        along(z, NZ, visit, here)
+
+    def t_others(send):
+        def visit(yi):
+            send(2 * yi)
+            send(2 * yi + 1)
+
+        along(y, NY, visit, lambda: send(2 * y + 1 - c))
 
     def put28(k, arr):
         for g in range(4):
@@ -377,14 +461,12 @@
         )
 
     def send28(k):
-        def one(j, carry):
-            @pl.when(j != dp)
+        def one(j):
+            @pl.when(j < 28)
             def _():
                 rcopy(P28.at[k, j], R28.at[k, dp], cs.at[k, 0], cr.at[k, 0], (j, t)).start()
 
-            return carry
-
-        lax.fori_loop(0, 28, one, 0)
+        dp_others(one)
 
         @pl.when(dp < 28)
         def _():
@@ -396,14 +478,10 @@
             drain(R28.at[k, pl.ds(0, 31)], cr.at[k, 0])
             L28[k, dp] = jnp.sum(R28[k], axis=0)
 
-            def one(j, carry):
-                @pl.when(j != dp)
-                def _():
-                    rcopy(L28.at[k, dp], L28.at[k, dp], cs.at[k, 1], cr.at[k, 1], (j, t)).start()
-
-                return carry
-
-            lax.fori_loop(0, NDP, one, 0)
+            def one(j):
+                rcopy(L28.at[k, dp], L28.at[k, dp], cs.at[k, 1], cr.at[k, 1], (j, t)).start()
+
+            dp_others(one)
 
     def end28(k):
         @pl.when(dp < 28)
@@ -434,14 +512,10 @@
             drain(R8T.at[k, pl.ds(0, 15)], cr.at[k, 2])
             R8D[k, dp] = jnp.sum(R8T[k], axis=0)
 
-            def one(j, carry):
-                @pl.when(j != dp)
-                def _():
-                    rcopy(R8D.at[k, dp], R8D.at[k, dp], cs.at[k, 3], cr.at[k, 3], (j, t)).start()
-
-                return carry
-
-            lax.fori_loop(0, NDP, one, 0)
+            def one(j):
+                rcopy(R8D.at[k, dp], R8D.at[k, dp], cs.at[k, 3], cr.at[k, 3], (j, t)).start()
+
+            dp_others(one)
 
     def reduce8(k):
         @pl.when(t < 8)
@@ -449,14 +523,10 @@
             drain(R8D.at[k, pl.ds(0, 31)], cr.at[k, 3])
             L8[k, t] = jnp.sum(R8D[k], axis=0)
 
-            def one(j, carry):
-                @pl.when(j != t)
-                def _():
-                    rcopy(L8.at[k, t], L8.at[k, t], cs.at[k, 4], cr.at[k, 4], (dp, j)).start()
-
-                return carry
-
-            lax.fori_loop(0, NT, one, 0)
+            def one(j):
+                rcopy(L8.at[k, t], L8.at[k, t], cs.at[k, 4], cr.at[k, 4], (dp, j)).start()
+
+            t_others(one)
 
     def end8(k):
         @pl.when(t < 8)
@@ -467,39 +537,57 @@
         def _():
             drain(L8.at[k, pl.ds(0, 8)], cr.at[k, 4])
 
-    hq = dot_nt(UQ[...], hidden.astype(F32), HI)
-    put8(0, AU[...] + dot_nn(hq, WIN[0].astype(F32), HI) * grad_scale)
+    add_up(1)
+    put8(0, AU[...])
     send8(0)
-    put28(0, AD[...] + dot_nn(GQ[...], act.astype(F32), HI) * grad_scale)
+    add_down(1)
+    put28(0, AD[...])
     send28(0)
-
-    def h_copy(i):
-        own = HG.at[x]
-        src = (own, own, HG.at[xl, top], HG.at[xrr, bot])[i]
-        return rcopy(src, src, hs.at[i], hr.at[i], at_x(xrr if i % 2 == 0 else xl))
-
-    def h_wait(i):
-        x2 = wrap(x + 2, NX)
-        ref = (HG.at[xl], HG.at[xrr], HG.at[x2, top], HG.at[x2, bot])[i]
-        rcopy(ref, ref, hs.at[i], hr.at[i], (dp, t)).wait_recv()
 
     def ig_product(i):
         IGP[i] = dot_nt(HG[i], WU[...].reshape(NZ * 128, WU.shape[2])).astype(BF16)
 
-    h_copy(0).start()
-    h_copy(1).start()
-    MU[...] += dot_nn(WIN[0].T, hidden) * grad_scale
-    MD[...] += dot_nn(act.T, WIN[1]) * grad_scale
+    h_copy(1, 0).start()
+    h_copy(1, 1).start()
+    MU[...] += dot_nn(WIN[0].T, HG[x]) * grad_scale
+    MD[...] += dot_nn(ACT[...].T, WIN[1]) * grad_scale
     store_u = pltpu.make_async_copy(MU, mu_out, acc_sem.at[0])
     store_d = pltpu.make_async_copy(MD, md_out, acc_sem.at[1])
     store_u.start()
     store_d.start()
+    for mat in range(2):
+        for g in range(2):
+            for step in range(1, 5):
+                for way in ring_ways(step, g):
+                    ring(mat, way, step, g).wait_send()
+            for i in range(6):
+                rs_copy(mat, g, i).wait_send()
+    for arr in range(2):
+        for h in range(2):
+
+            @pl.when(foreign(h))
+            def _():
+                piece(arr, h).wait_send()
+
+        for off in range(1, NY):
+            spread(arr, off).wait_send()
+        for off in range(NY):
+            to_sibling(arr, wrap(y - off, NY), off).wait_send()
+
+    @pl.when(t == 0)
+    def _():
+        for arr in range(2):
+
+            def one(j, carry):
+                rcopy(WIN.at[arr], WIN.at[arr], ws.at[arr], wr.at[arr], (dp, j)).wait_send()
+                return carry
+
+            lax.fori_loop(1, NT, one, 0)
+
+    h_relay(0)
     middle8(0)
     reduce28(0)
-    h_wait(0)
-    h_copy(2).start()
-    h_wait(1)
-    h_copy(3).start()
+    h_relay(1)
 
     def ig_near(d, carry):
         ig_product(wrap(x + d - 1, NX))
@@ -507,8 +595,9 @@
 
     lax.fori_loop(0, 3, ig_near, 0)
     reduce8(0)
-    h_wait(2)
-    h_wait(3)
+    for g in range(2):
+        h_wait(g, 2)
+        h_wait(g, 3)
     lax.fori_loop(3, 4, ig_near, 0)
     other = IGP.at[pl.ds(2 - 2 * c, 2)]
     pair_copy = rcopy(other, IGX, ps_s.at[0], ps_r.at[0], sib)
@@ -521,14 +610,10 @@
     gram_part = dot_nt(down_sum, down_sum, HI)
     GR[t] = jnp.concatenate([gram_part[8 * g : 8 * g + 8] for g in range(4)], axis=1)
 
-    def gram_send(j, carry):
-        @pl.when(j != t)
-        def _():
-            rcopy(GR.at[t], GR.at[t], gs.at[0], gr.at[0], (dp, j)).start()
-
-        return carry
-
-    lax.fori_loop(0, NT, gram_send, 0)
+    def gram_send(j):
+        rcopy(GR.at[t], GR.at[t], gs.at[0], gr.at[0], (dp, j)).start()
+
+    t_others(gram_send)
 
     pair_copy.wait_recv()
     for i in range(2):
@@ -537,12 +622,10 @@
             PS[k, i] = both[:, k * 128 : (k + 1) * 128]
     RY[y] = PS[y]
 
-    def ry_send(off, carry):
-        j = wrap(y + off, NY)
+    def ry_send(j):
         rcopy(PS.at[j], RY.at[y], ry_s.at[0], ry_r.at[0], (dp, 2 * j + c)).start()
-        return carry
-
-    lax.fori_loop(1, NY, ry_send, 0)
+
+    along(y, NY, ry_send, lambda: None)
 
     end8(0)
     up_sum = get(L8, 0, 2)
@@ -550,6 +633,26 @@
     send28(1)
     middle8(1)
 
+    def sums_left(k):
+        @pl.when(dp < 28)
+        def _():
+            drain(P28.at[k, pl.ds(0, 27)], cs.at[k, 0])
+            drain(R28.at[k, pl.ds(0, 31)], cs.at[k, 1])
+
+        @pl.when(dp >= 28)
+        def _():
+            drain(P28.at[k, pl.ds(0, 28)], cs.at[k, 0])
+
+        @pl.when(t < 8)
+        def _():
+            drain(P8.at[k, pl.ds(0, 7)], cs.at[k, 2])
+            drain(R8D.at[k, pl.ds(0, 31)], cs.at[k, 3])
+            drain(R8T.at[k, pl.ds(0, 15)], cs.at[k, 4])
+
+        @pl.when(t >= 8)
+        def _():
+            drain(P8.at[k, pl.ds(0, 8)], cs.at[k, 2])
+
     def put_out(ref, value, dst, i):
         ref[...] = value
         copy = pltpu.make_async_copy(ref, dst, out_sem.at[i])
@@ -559,6 +662,13 @@
     results = []
     up_inv = inverse_factor(dot_nt(up_sum, up_sum, HI))
     results.append(put_out(UL, dot_nn(up_inv, up_sum, HI), ul_out, 0))
+    store_u.wait()
+    store_d.wait()
+    sums_left(0)
+    for g in range(2):
+        for i in range(4):
+            h_copy(g, i).wait_send()
+    pair_copy.wait_send()
     reduce28(1)
     drain(GR.at[pl.ds(0, NT - 1)], gr.at[0])
     packed = jnp.sum(GR[...], axis=0)
@@ -611,38 +721,6 @@
         put_out(DR, dot_nn(down_inv, get(L8, 1, 2), HI) * (1.0 / NDP), dr_out, 3)
     )
 
-    for mat in range(2):
-        for g in range(2):
-            for step in range(1, 5):
-                for way in ring_ways(step, g):
-                    ring(mat, way, step, g).wait_send()
-            for i in range(6):
-                rs_copy(mat, g, i).wait_send()
-    for arr in range(2):
-        for h in range(2):
-
-            @pl.when(foreign(h))
-            def _():
-                piece(arr, h).wait_send()
-
-        for off in range(1, NY):
-            spread(arr, off).wait_send()
-        for off in range(NY):
-            to_sibling(arr, wrap(y - off, NY), off).wait_send()
-
-    @pl.when(t == 0)
-    def _():
-        for arr in range(2):
-
-            def one(j, carry):
-                rcopy(WIN.at[arr], WIN.at[arr], ws.at[arr], wr.at[arr], (dp, j)).wait_send()
-                return carry
-
-            lax.fori_loop(1, NT, one, 0)
-
-    for i in range(4):
-        h_copy(i).wait_send()
-    pair_copy.wait_send()
     drain(PS.at[pl.ds(0, NY - 1)], ry_s.at[0])
     for i in range(2):
 
@@ -650,30 +728,8 @@
         def _():
             rcopy(FY.at[i], FY.at[i], fs.at[i], fr.at[i], (dp, t)).wait_send()
 
-    for k in range(2):
-
-        @pl.when(dp < 28)
-        def _():
-            drain(P28.at[k, pl.ds(0, 27)], cs.at[k, 0])
-            drain(R28.at[k, pl.ds(0, 31)], cs.at[k, 1])
-
-        @pl.when(dp >= 28)
-        def _():
-            drain(P28.at[k, pl.ds(0, 28)], cs.at[k, 0])
-
-        @pl.when(t < 8)
-        def _():
-            drain(P8.at[k, pl.ds(0, 7)], cs.at[k, 2])
-            drain(R8D.at[k, pl.ds(0, 31)], cs.at[k, 3])
-            drain(R8T.at[k, pl.ds(0, 15)], cs.at[k, 4])
-
-        @pl.when(t >= 8)
-        def _():
-            drain(P8.at[k, pl.ds(0, 8)], cs.at[k, 2])
-
+    sums_left(1)
     drain(GR.at[pl.ds(0, NT - 1)], gs.at[0])
-    store_u.wait()
-    store_d.wait()
     for copy in results:
         copy.wait()
 
@@ -689,7 +745,7 @@
     for i, low, high in ((5, 1, 2), (6, 3, 4)):
         for k in (low, high, i):
             loads[k].wait()
-        held[i][...] -= dot_nn(held[low][...].T, held[high][...], HI)
+        held[i][...] -= dot_thirds(held[low][...], held[high][...])
         for k in (i, low, high):
             stores[k].start()
     loads[0].wait()
@@ -723,6 +779,7 @@
         out_specs=[hbm] * 7,
         scratch_shapes=[
             V((2, rows, feats), BF16),
+            V((rows, hid), BF16),
             V((rank, hid), F32),
             V((rank, win), F32),
             V((rank, win), F32),
@@ -772,8 +829,8 @@
             sem((2,)),
             sem((2, 2, 6)),
             sem((2, 2, 6)),
-            sem((4,)),
-            sem((4,)),
+            sem((2, 4)),
+            sem((2, 4)),
             sem((1,)),
             sem((1,)),
             sem((1,)),

time: 116 us -> 110 us (0.948)
  Pallas kernels: 115 us -> 109 us
    pallas_call x1, Pallas kernels: 110 us -> 106 us  [shards(): pl.pallas_call(kernel, out_shape=[shape((rows, feats), BF16), shape((rank...]
    pallas_call x1, Pallas kernels: 4.41 us -> 3.1 us  [shards(): pl.pallas_call(finish, out_shape=[shape((rows, feats), BF16), shape((rank...]
where the time goes in v3:
time: 110 us
  Pallas kernels  109 us (99%)
    pallas_call x1, Pallas kernels, shards(): pl.pallas_call(kernel, out_shape=[shape((rows, feats), BF16), shape((rank...  106 us
    pallas_call x1, Pallas kernels, shards(): pl.pallas_call(finish, out_shape=[shape((rows, feats), BF16), shape((rank...  3.1 us

profile of v3, /device:TPU:1, one launch (start us, length us, event | category | flops | bytes accessed | tf_op | source)
XLA Modules:
  0.0 109.6 jit_solution(13321064038451125097)
XLA Ops:
  0.6 105.9 %shard_map.135 = (bf16[128,256]{1,0:T(8,128)(2,1)}, f32[32,256]{1,0:T(8,128)}, f32[32,896]{1,0:T(8,128)}, f32[32,896]{1,0:T(8,128)}, f32[32,256]{1,0:T(8,128)}, /*index=5*/f32[256,896]{1,0:T(8,128)}, f32[896,256]{1,0:T(8,128)}) custom-call(bf16[128,256]{1,0:T(8,128)(2,1)} %tok_in.1, bf16[128,256]{1,0:T(8,128)(2,1)} %og_in.1, bf16[128,896]{1,0:T(8,128)(2,1)} %wu_in.1, ...), custom_call_target="tpu_custom_call" | custom-call | tf_op jit(solution)/shard_map/pallas_call | solution.py:767
  106.5 3.1 %shard_map.136 = (bf16[128,256]{1,0:T(8,128)(2,1)}, f32[32,256]{1,0:T(8,128)}, f32[32,896]{1,0:T(8,128)}, f32[32,896]{1,0:T(8,128)}, f32[32,256]{1,0:T(8,128)}, ...) custom-call(bf16[128,256]{1,0:T(8,128)(2,1)} %get-tuple-element.21.refs_0_, f32[32,256]{1,0:T(8,128)} %get-tuple-element.22.refs_1_, ...), custom_call_target="tpu_custom_call" | custom-call | tf_op jit(solution)/shard_map/pallas_call | solution.py:850

commit v4 on v3

--- a/solution.py
+++ b/solution.py
@@ -143,8 +143,6 @@
                 device_id_type=MESH,
             )
 
-    pl.semaphore_wait(barrier, NDP + NT - 2 + 2 * jnp.where(mine, 0, 1).astype(jnp.int32))
-
     for load in loads[:4]:
         load.wait()
     for h in range(2):
@@ -157,6 +155,8 @@
     @pl.when(t == 0)
     def _():
         WIN[...] = TO[...]
+
+    pl.semaphore_wait(barrier, NDP + NT - 2 + 2 * jnp.where(mine, 0, 1).astype(jnp.int32))
 
     def slot(mat, zi, g):
         hidden_range = pl.ds(*GROUPS[g])
@@ -191,6 +191,10 @@
             ring_arrived(mat, way, step - 1, g)
             if way in ring_ways(step, g):
                 ring(mat, way, step, g).start()
+
+    def ring_hop(mat, way, step, g):
+        ring_arrived(mat, way, step - 1, g)
+        ring(mat, way, step, g).start()
 
     def ring_end(mat, g):
         for way in ring_ways(4, g):
@@ -324,30 +328,38 @@
     AU[...] = dot_nt(UQ[...], MU[...], HI)
     ring_pass(0, 3, 0)
     ring_pass(1, 3, 0)
-    ring_send(0, 1, 1)
+    for mat in range(2):
+        ring(mat, 1, 1, 1).start()
     loads[5].wait()
     load_d.wait()
     AD[...] = dot_nt(DQ[...], MD[...], HI)
-    ring_pass(0, 4, 0)
-    ring_pass(1, 4, 0)
-    ring_send(1, 1, 1)
+    for mat in range(2):
+        ring_hop(mat, 0, 4, 0)
+    for mat in range(2):
+        ring_arrived(mat, 1, 3, 0)
+    for mat in range(2):
+        ring(mat, 0, 1, 1).start()
     y_arrivals(0)
-    ring_pass(0, 2, 1)
+    for mat in range(2):
+        ring_hop(mat, 1, 2, 1)
     ring_end(0, 0)
     sibling_arrivals(0)
     products(0, 0)
     rs_first(0, 0)
-    ring_pass(1, 2, 1)
+    ring_hop(0, 1, 3, 1)
+    ring_end(1, 0)
+    ring_hop(1, 1, 3, 1)
+    for mat in range(2):
+        ring_hop(mat, 0, 2, 1)
     y_arrivals(1)
-    ring_pass(0, 3, 1)
-    ring_end(1, 0)
     sibling_arrivals(1)
     products(1, 0)
     rs_first(1, 0)
     rs_second(0, 0)
-    ring_pass(1, 3, 1)
-    ring_pass(0, 4, 1)
-    ring_pass(1, 4, 1)
+    for mat in range(2):
+        ring_hop(mat, 1, 4, 1)
+    for mat in range(2):
+        ring_hop(mat, 0, 3, 1)
 
     @pl.when(t != 0)
     def _():
@@ -394,9 +406,11 @@
         h_wait(g, 1)
         h_copy(g, 3).start()
 
+    ring_arrived(0, 0, 3, 1)
     ring_end(0, 1)
     products(0, 1)
     rs_first(0, 1)
+    ring_arrived(1, 0, 3, 1)
     ring_end(1, 1)
     products(1, 1)
     rs_first(1, 1)
@@ -593,15 +607,33 @@
         ig_product(wrap(x + d - 1, NX))
         return carry
 
+    order = (1 - lax.rem(x, 2), lax.rem(x, 2))
+
+    def pair_copy(k):
+        i = order[k]
+        return rcopy(IGP.at[2 - 2 * c + i], IGX.at[i], ps_s.at[k], ps_r.at[k], sib)
+
+    def pair_sum(k):
+        i = order[k]
+        rcopy(IGX.at[i], IGX.at[i], ps_s.at[k], ps_r.at[k], sib).wait_recv()
+        both = (IGP[2 * c + i].astype(F32) + IGX[i].astype(F32)).astype(BF16)
+        for j in range(NY):
+            PS[k, j] = both[:, j * 128 : (j + 1) * 128]
+        RY[k, y] = PS[k, y]
+
+        def ry_send(j):
+            rcopy(PS.at[k, j], RY.at[k, y], ry_s.at[k], ry_r.at[k], (dp, 2 * j + c)).start()
+
+        along(y, NY, ry_send, lambda: None)
+
     lax.fori_loop(0, 3, ig_near, 0)
+    pair_copy(0).start()
     reduce8(0)
     for g in range(2):
         h_wait(g, 2)
         h_wait(g, 3)
     lax.fori_loop(3, 4, ig_near, 0)
-    other = IGP.at[pl.ds(2 - 2 * c, 2)]
-    pair_copy = rcopy(other, IGX, ps_s.at[0], ps_r.at[0], sib)
-    pair_copy.start()
+    pair_copy(1).start()
 
     end28(0)
     down_sum = get(L28, 0, 7)
@@ -615,18 +647,8 @@
 
     t_others(gram_send)
 
-    pair_copy.wait_recv()
-    for i in range(2):
-        both = (IGP[2 * c + i].astype(F32) + IGX[i].astype(F32)).astype(BF16)
-        for k in range(NY):
-            PS[k, i] = both[:, k * 128 : (k + 1) * 128]
-    RY[y] = PS[y]
-
-    def ry_send(j):
-        rcopy(PS.at[j], RY.at[y], ry_s.at[0], ry_r.at[0], (dp, 2 * j + c)).start()
-
-    along(y, NY, ry_send, lambda: None)
-
+    pair_sum(0)
+    pair_sum(1)
     end8(0)
     up_sum = get(L8, 0, 2)
     put28(1, dot_nn(up_sum, MU[...], HI))
@@ -668,7 +690,8 @@
     for g in range(2):
         for i in range(4):
             h_copy(g, i).wait_send()
-    pair_copy.wait_send()
+    pair_copy(0).wait_send()
+    pair_copy(1).wait_send()
     reduce28(1)
     drain(GR.at[pl.ds(0, NT - 1)], gr.at[0])
     packed = jnp.sum(GR[...], axis=0)
@@ -677,9 +700,9 @@
     down_inv = inverse_factor(gram)
     results.append(put_out(DL, dot_nn(down_inv, down_sum, HI), dl_out, 1))
 
-    drain(RY.at[pl.ds(0, NY - 1)], ry_r.at[0])
-    for i in range(2):
-        FY[i] = jnp.sum(RY[:, i].astype(F32), axis=0).astype(BF16)
+    for k in range(2):
+        drain(RY.at[k, pl.ds(0, NY - 1)], ry_r.at[k])
+        FY[order[k]] = jnp.sum(RY[k].astype(F32), axis=0).astype(BF16)
 
     def last(i, h):
         return rcopy(
@@ -705,6 +728,15 @@
     results.append(
         put_out(UR, dot_nn(up_inv, get(L28, 1, 7), HI) * (1.0 / NDP), ur_out, 2)
     )
+    end8(1)
+    results.append(
+        put_out(DR, dot_nn(down_inv, get(L8, 1, 2), HI) * (1.0 / NDP), dr_out, 3)
+    )
+
+    for k in range(2):
+        drain(PS.at[k, pl.ds(0, NY - 1)], ry_s.at[k])
+    sums_left(1)
+    drain(GR.at[pl.ds(0, NT - 1)], gs.at[0])
     for h in range(2):
 
         @pl.when(foreign(h))
@@ -716,20 +748,12 @@
         )
         copy.start()
         results.append(copy)
-    end8(1)
-    results.append(
-        put_out(DR, dot_nn(down_inv, get(L8, 1, 2), HI) * (1.0 / NDP), dr_out, 3)
-    )
-
-    drain(PS.at[pl.ds(0, NY - 1)], ry_s.at[0])
     for i in range(2):
 
         @pl.when(foreign(i))
         def _():
             rcopy(FY.at[i], FY.at[i], fs.at[i], fr.at[i], (dp, t)).wait_send()
 
-    sums_left(1)
-    drain(GR.at[pl.ds(0, NT - 1)], gs.at[0])
     for copy in results:
         copy.wait()
 
@@ -800,8 +824,8 @@
             V((NX, rows, hid), BF16),
             V((NX, rows, quarter), BF16),
             V((2, rows, quarter), BF16),
-            V((NY, 2, rows, 128), BF16),
-            V((NY, 2, rows, 128), BF16),
+            V((2, NY, rows, 128), BF16),
+            V((2, NY, rows, 128), BF16),
             V((2, rows, 128), BF16),
             V((2, rows, 128), BF16),
             V((win, hid), F32),
@@ -831,10 +855,10 @@
             sem((2, 2, 6)),
             sem((2, 4)),
             sem((2, 4)),
-            sem((1,)),
-            sem((1,)),
-            sem((1,)),
-            sem((1,)),
+            sem((2,)),
+            sem((2,)),
+            sem((2,)),
+            sem((2,)),
             sem((2,)),
             sem((2,)),
             sem((2, 5)),

time: 110 us -> 107 us (0.973)
  Pallas kernels: 109 us -> 106 us
    pallas_call x1, Pallas kernels: 106 us -> 103 us  [shards(): pl.pallas_call(kernel, out_shape=[shape((rows, feats), BF16), shape((rank...]
where the time goes in v4:
time: 107 us
  Pallas kernels  106 us (99%)
    pallas_call x1, Pallas kernels, shards(): pl.pallas_call(kernel, out_shape=[shape((rows, feats), BF16), shape((rank...  103 us
    pallas_call x1, Pallas kernels, shards(): pl.pallas_call(finish, out_shape=[shape((rows, feats), BF16), shape((rank...  3.1 us

profile of v4, /device:TPU:1, one launch (start us, length us, event | category | flops | bytes accessed | tf_op | source)
XLA Modules:
  0.0 106.6 jit_solution(3957300919317107402)
XLA Ops:
  0.6 102.9 %shard_map.135 = (bf16[128,256]{1,0:T(8,128)(2,1)}, f32[32,256]{1,0:T(8,128)}, f32[32,896]{1,0:T(8,128)}, f32[32,896]{1,0:T(8,128)}, f32[32,256]{1,0:T(8,128)}, /*index=5*/f32[256,896]{1,0:T(8,128)}, f32[896,256]{1,0:T(8,128)}) custom-call(bf16[128,256]{1,0:T(8,128)(2,1)} %tok_in.1, bf16[128,256]{1,0:T(8,128)(2,1)} %og_in.1, bf16[128,896]{1,0:T(8,128)(2,1)} %wu_in.1, ...), custom_call_target="tpu_custom_call" | custom-call | tf_op jit(solution)/shard_map/pallas_call | solution.py:791
  103.5 3.1 %shard_map.136 = (bf16[128,256]{1,0:T(8,128)(2,1)}, f32[32,256]{1,0:T(8,128)}, f32[32,896]{1,0:T(8,128)}, f32[32,896]{1,0:T(8,128)}, f32[32,256]{1,0:T(8,128)}, ...) custom-call(bf16[128,256]{1,0:T(8,128)(2,1)} %get-tuple-element.21.refs_0_, f32[32,256]{1,0:T(8,128)} %get-tuple-element.22.refs_1_, ...), custom_call_target="tpu_custom_call" | custom-call | tf_op jit(solution)/shard_map/pallas_call | solution.py:874

commit v5 on v4

--- a/solution.py
+++ b/solution.py
@@ -551,12 +551,12 @@
         def _():
             drain(L8.at[k, pl.ds(0, 8)], cr.at[k, 4])
 
+    add_down(1)
+    put28(0, AD[...])
+    send28(0)
     add_up(1)
     put8(0, AU[...])
     send8(0)
-    add_down(1)
-    put28(0, AD[...])
-    send28(0)
 
     def ig_product(i):
         IGP[i] = dot_nt(HG[i], WU[...].reshape(NZ * 128, WU.shape[2])).astype(BF16)

time: 107 us -> 107 us (level)
  no operation moved by 1% of the time
where the time goes in v5:
time: 107 us
  Pallas kernels  107 us (100%)
    pallas_call x1, Pallas kernels, shards(): pl.pallas_call(kernel, out_shape=[shape((rows, feats), BF16), shape((rank...  103 us
    pallas_call x1, Pallas kernels, shards(): pl.pallas_call(finish, out_shape=[shape((rows, feats), BF16), shape((rank...  3.11 us

profile of v5, /device:TPU:1, one launch (start us, length us, event | category | flops | bytes accessed | tf_op | source)
XLA Modules:
  0.0 107.2 jit_solution(17906718168373780762)
XLA Ops:
  0.6 103.4 %shard_map.135 = (bf16[128,256]{1,0:T(8,128)(2,1)}, f32[32,256]{1,0:T(8,128)}, f32[32,896]{1,0:T(8,128)}, f32[32,896]{1,0:T(8,128)}, f32[32,256]{1,0:T(8,128)}, /*index=5*/f32[256,896]{1,0:T(8,128)}, f32[896,256]{1,0:T(8,128)}) custom-call(bf16[128,256]{1,0:T(8,128)(2,1)} %tok_in.1, bf16[128,256]{1,0:T(8,128)(2,1)} %og_in.1, bf16[128,896]{1,0:T(8,128)(2,1)} %wu_in.1, ...), custom_call_target="tpu_custom_call" | custom-call | tf_op jit(solution)/shard_map/pallas_call | solution.py:791
  104.1 3.1 %shard_map.136 = (bf16[128,256]{1,0:T(8,128)(2,1)}, f32[32,256]{1,0:T(8,128)}, f32[32,896]{1,0:T(8,128)}, f32[32,896]{1,0:T(8,128)}, f32[32,256]{1,0:T(8,128)}, ...) custom-call(bf16[128,256]{1,0:T(8,128)(2,1)} %get-tuple-element.21.refs_0_, f32[32,256]{1,0:T(8,128)} %get-tuple-element.22.refs_1_, ...), custom_call_target="tpu_custom_call" | custom-call | tf_op jit(solution)/shard_map/pallas_call | solution.py:874
